TPU v7x, 256 devices: a 2x2x32 block of a 4x8x32 slice. The times are simulated.
256 devices in a mesh: parts: 4 (over y, x), rows: 64 (over z, core).
Axes of the slice: x: 2, y: 2, z: 32, core: 2. Of those that a mesh axis runs over, the one named last changes fastest.
The devices are a block of a 4x8x32 slice.
Arguments:
- features: bfloat16 [1024, 256, 512], P(('parts', 'rows')), parts along dimension 0, may hold values from -10 to 10, as said below
- grad_out: bfloat16 [1024, 256, 512], P(('parts', 'rows')), parts along dimension 0, may hold values from -11 to 11, as said below
- filters: bfloat16 [512, 3, 3, 512], replicated, may hold values from -0.09375 to 0.09375
- norm_gain: float32 [512], replicated, may hold values from 0.25 to 1.75
- norm_bias: float32 [512], replicated, may hold values from -1 to 1
Outputs:
- grad_in: bfloat16 [1024, 256, 512], P(('parts', 'rows')), parts along dimension 0
- filter_grad: float32 [2048, 3, 3, 512], P(('parts', 'rows')), parts along dimension 0
- gain_grad: float32 [2048], P('parts'), parts along dimension 0
- bias_grad: float32 [2048], P('parts'), parts along dimension 0
There are 4 independent parts, one for each index of `parts`. A program takes and returns all parts, laid end to end along the dimension named above; an argument that names none is the same for every part. Nothing has to cross between parts.
Inputs may be any that keep to these rules, and one draw needn't show every extreme that they name: `features`: each image row has its own offset and spread for each group. `grad_out`: each image row and channel has its own offset.
All inputs are finite; a program needn't handle non-finite values.
Results may differ from a plain program's by a relative error of at most 0.0005.
Values may be sent and summed in bfloat16 or wider, within the bound.
No kernel may reach another device: no remote copies, remote signals or barrier semaphores. Data moves between devices by JAX's collectives and lax.ppermute only.
A program may use at most 128 MiB of HBM per device.

v0:
```python
import jax
import jax.numpy as jnp
from jax import lax
from jax.sharding import Mesh
from jax.sharding import PartitionSpec as P

GROUPS = 32
ROWS = ("rows_0", "rows_1")
PARTS_ROWS = ("parts", "rows_0", "rows_1")


epsilon = 1e-06


def copy_for_each(shard, axis):
    copies = jnp.broadcast_to(shard, (lax.axis_size(axis), *shard.shape))
    return lax.all_to_all(copies, axis, split_axis=0, concat_axis=0, tiled=True)


def of_everyone(shard, axis):
    return copy_for_each(shard, axis).sum(axis=0)


def in_one(arrays, axis):
    vector, at, done = (jnp.concatenate([a.reshape(-1) for a in arrays]), 0, [])
    total = of_everyone(vector, axis)
    for a in arrays:
        done.append(total[at : at + a.size].reshape(a.shape))
        at += a.size
    return tuple(done)


def padded_2(block, sides, width):
    for axis, dim in sides:
        count = lax.axis_size(axis)
        forward = [(i, i + 1) for i in range(count - 1)]
        backward = [(target, source) for source, target in forward]
        low = lax.ppermute(
            lax.slice_in_dim(block, block.shape[dim] - width, None, axis=dim), axis, forward
        )
        high = lax.ppermute(lax.slice_in_dim(block, 0, width, axis=dim), axis, backward)
        block = jnp.concatenate([low, block, high], axis=dim)
    return block


def own_block(parts, axes, order):
    inside = parts.shape[1:]
    parts = parts.reshape(*(lax.axis_size(a) for a in axes), *inside)
    parts = jnp.moveaxis(parts, order, range(len(axes))).reshape(-1, *inside)
    for k in order:
        parts = lax.psum_scatter(parts, axes[k], scatter_dimension=0, tiled=True)
    return parts[0]


def cut_along(shard, dim, peers):
    dims = shard.shape
    parts = shard.reshape(*dims[:dim], peers, dims[dim] // peers, *dims[dim + 1 :])
    return jnp.moveaxis(parts, dim, 0)


def summed_rows(shard, axes, order, dim):
    peers = lax.axis_size(axes)
    return own_block(cut_along(shard, dim, peers), axes, order)


def over_axes(shard, axes):
    for axis in axes:
        shard = lax.psum(shard, axis)
    return shard


def expand(values, channels):
    groups = values.shape[0]
    return jnp.broadcast_to(values[:, None], (groups, channels // groups)).reshape(channels)


def group_total(values):
    return values.reshape(GROUPS, -1).sum(axis=1)


def local(features, grad_out, filters, norm_gain, norm_bias):
    height, columns, channels = features.shape
    devices = lax.axis_size(ROWS)
    pixels = height * devices * columns
    members = pixels * (channels // GROUPS)
    widened = features.astype(jnp.float32)
    partial_value = jnp.sum(widened, axis=(0, 1))
    squares = jnp.sum(widened * widened, axis=(0, 1))
    summed, summed_sq = in_one((group_total(partial_value), group_total(squares)), ROWS)
    group_mean = summed / members
    group_var = summed_sq / members - group_mean * group_mean
    centered = widened - expand(group_mean, channels)
    inv_std = lax.rsqrt(group_var + epsilon)
    normalized = centered * expand(inv_std, channels)
    normed = normalized * norm_gain + norm_bias
    sigmoid_z = jax.nn.sigmoid(normed)
    activation = (normed * sigmoid_z).astype(jnp.bfloat16)
    flat_act = activation.reshape(-1, channels)
    extended = padded_2(grad_out, ((ROWS, 0),), 1)
    padded = jnp.pad(extended, ((0, 0), (1, 1), (0, 0)))
    windows = []
    grad_act = jnp.zeros((height * columns, channels), jnp.float32)
    for tap_row in range(3):
        for tap_col in range(3):
            window = padded[
                2 - tap_row : 2 - tap_row + height, 2 - tap_col : 2 - tap_col + columns
            ].reshape(-1, channels)
            windows.append(window)
            grad_act = grad_act + jnp.dot(
                window, filters[:, tap_row, tap_col, :], preferred_element_type=jnp.float32
            )
    pieces = []
    for window in windows:
        pieces.append(
            lax.dot_general(
                window, flat_act, (((0,), (0,)), ((), ())), preferred_element_type=jnp.float32
            )
        )
    filter_grad = summed_rows(
        jnp.stack(pieces, axis=1).reshape(channels, 3, 3, channels) / pixels, ROWS, (1, 0), 0
    )
    grad_pre = grad_act.reshape(height, columns, channels) * (
        sigmoid_z * (1.0 + normed * (1.0 - sigmoid_z))
    )
    bias_part = jnp.sum(grad_pre, axis=(0, 1))
    gain_part = jnp.sum(grad_pre * normalized, axis=(0, 1))
    gain_grad, bias_grad = (over_axes(gain_part, ROWS), over_axes(bias_part, ROWS))
    mean_grad = group_total(norm_gain * bias_grad) / members
    mean_cross = group_total(norm_gain * gain_grad) / members
    grad_in = expand(inv_std, channels) * (
        grad_pre * norm_gain
        - expand(mean_grad, channels)
        - normalized * expand(mean_cross, channels)
    )
    return (grad_in.astype(jnp.bfloat16), filter_grad, gain_grad, bias_grad)


def solution(mesh):
    torus = Mesh(mesh.devices.reshape(mesh.shape["parts"], 32, 2), ("parts", "rows_0", "rows_1"))
    in_specs = (P(PARTS_ROWS, None, None), P(PARTS_ROWS, None, None), P(), P(), P())
    out_specs = (P(PARTS_ROWS, None, None), P(PARTS_ROWS, None, None, None), P("parts"), P("parts"))
    return jax.shard_map(local, mesh=torus, in_specs=in_specs, out_specs=out_specs, check_vma=False)
```

profile of v0, /device:TPU:38, one launch (start us, length us, event | category | flops | bytes accessed | tf_op | source)
XLA Modules:
  0.0 278.2 jit_solution(3158949779627645872)
XLA Ops:
  9.9 34.2 %all-to-all-start = ((f32[64,1,64]{2,1,0:T(1,128)}), f32[64,1,64]{2,1,0:T(1,128)S(1)}, u32[]{:S(2)}, u32[]{:S(2)}) async-start(f32[64,1,64]{2,1,0:T(1,128)} %broadcast_in_dim.10), calls=%async_computation | async-start | bytes 65536 | tf_op jit(solution)/shard_map/all_to_all | solution.py:17
  48.4 17.7 %all-to-all-done = f32[64,1,64]{2,1,0:T(1,128)S(1)} async-done(((f32[64,1,64]{2,1,0:T(1,128)}), f32[64,1,64]{2,1,0:T(1,128)S(1)}, u32[]{:S(2)}, u32[]{:S(2)}) %all-to-all-start) | async-done | bytes 16416 | tf_op jit(solution)/shard_map/all_to_all | solution.py:17
  67.2 2.8 %fusion.5 = bf16[6,258,512]{1,2,0:T(8,128)(2,1)S(1)} fusion(bf16[1,256,512]{1,2,0:T(8,128)(2,1)} %collective-permute-done.1, bf16[4,256,512]{1,2,0:T(8,128)(2,1)S(1)} %copy.47, bf16[1,256,512]{1,2,0:T(8,128)(2,1)} %copy-done.14), kind=kLoop, calls=%fused_computation.11 | loop fusion | flops 9510912 | bytes 3158016 | tf_op jit(solution)/shard_map/concatenate | solution.py:42
  70.0 3.6 %fusion.34 = f32[512,9,512]{2,0,1:T(8,128)} fusion(bf16[6,258,512]{1,2,0:T(8,128)(2,1)S(1)} %fusion.5, bf16[4,256,512]{2,1,0:T(8,128)(2,1)} %param.5, f32[512]{0:T(512)S(1)} %copy-done.18, f32[512]{0:T(512)S(1)} %copy-done.17, f32[512]{0:T(512)S(1)} %sub.30, f32[512]{0:T(512)S(1)} %mul.69), kind=kOutput, calls=%fused_computation.50 | convolution fusion | flops 542113792 | bytes 3153920 | tf_op jit(solution)/shard_map/dot_general | solution.py:115
  73.6 3.1 %fusion.27 = f32[512,9,512]{2,0,1:T(8,128)} fusion(f32[512,9,512]{2,0,1:T(8,128)} %fusion.34, bf16[1,256,512]{1,2,0:T(8,128)(2,1)} %collective-permute-done.1, bf16[4,256,512]{1,2,0:T(8,128)(2,1)S(1)} %copy.47, bf16[4,256,512]{2,1,0:T(8,128)(2,1)S(1)} %copy-done, f32[512]{0:T(512)S(1)} %copy-done.18, f32[512]{0:T(512)S(1)} %copy-done.17, f32[512]{0:T(512)S(1)} %sub.30, ...), kind=kOutput, calls=%fused_computation.36 | convolution fusion | flops 544735232 | bytes 3416064 | tf_op jit(solution)/shard_map/dot_general | solution.py:115
  78.7 2.3 fusion.32
  81.0 2.2 fusion.31
  83.1 2.1 fusion.30
  85.2 2.3 fusion.29
  87.5 2.1 fusion.26
  89.6 2.1 fusion.28
  91.7 4.8 %broadcast_multiply_fusion = f32[512,9,512]{2,0,1:T(8,128)S(1)} fusion(f32[512,9,512]{2,0,1:T(8,128)} %fusion.28), kind=kLoop, calls=%fused_computation.2 | loop fusion | flops 2359296 | bytes 18874368 | tf_op jit(solution)/shard_map/div | solution.py:120
  96.5 4.9 %copy.61 = f32[2,32,8,3,3,512]{5,2,4,3,1,0:T(8,128)} copy(f32[2,32,8,3,3,512]{5,2,0,1,4,3:T(8,128)S(1)} %bitcast.103) | data formatting | bytes 18874368 | tf_op jit(solution)/shard_map/transpose | solution.py:49
  101.6 24.8 %reduce-scatter.3.cloned.1.call-done = f32[32,8,3,3,512]{4,1,3,2,0:T(8,128)} async-done(((f32[64,8,3,3,512]{4,1,3,2,0:T(8,128)}), f32[32,8,3,3,512]{4,1,3,2,0:T(8,128)}) %reduce-scatter.3.cloned.1.call-update) | async-done | bytes 4718608 | tf_op jit(solution)/shard_map/reduce_scatter | solution.py:51
  126.5 3.4 %fusion.48 = f32[1024,512]{1,0:T(8,128)} fusion(bf16[1024,512]{1,0:T(8,128)(2,1)} %bitcast.106, bf16[512,3,3,512]{3,0,2,1:T(8,128)(2,1)} %param.7), kind=kOutput, calls=%fused_computation.66 | convolution fusion | flops 536870912 | bytes 3670016 | tf_op jit(solution)/shard_map/dot_general | solution.py:109
  129.9 4.2 %fusion.86 = (bf16[4,256,512]{1,2,0:T(8,128)(2,1)}, bf16[4,256,512]{1,2,0:T(8,128)(2,1)}, bf16[4,256,512]{1,2,0:T(8,128)(2,1)}, bf16[4,256,512]{1,2,0:T(8,128)(2...) fusion(bf16[6,258,512]{1,2,0:T(8,128)(2,1)S(1)} %fusion.5), kind=kLoop, calls=%fused_computation.99 | loop fusion | bytes 12582912 | tf_op jit(solution)/shard_map/slice | solution.py:105
  134.1 2.4 copy.56
  137.7 2.4 copy.54
  144.3 2.5 pad_maximum_fusion.1
  146.8 2.4 copy.58
  149.2 2.3 copy.52
  164.0 58.2 %all-reduce.1 = (f32[512]{0:T(512)S(1)}, f32[512]{0:T(512)S(1)}) all-reduce(f32[512]{0:T(512)S(1)} %get-tuple-element.5, f32[512]{0:T(512)S(1)} %get-tuple-element.4), channel_id=1, replica_groups=mesh['parts'=4,'rows_0'=32,'rows_1'=2] {'rows_0'}, use_global_device_ids=true, to_apply=%region_10.11 | all-reduce | flops 1024 | bytes 8192 | tf_op jit(solution)/shard_map/psum | solution.py:68
  222.2 2.5 all-reduce.2
  227.0 44.3 %reduce-scatter.5.cloned.1.call-done = f32[1,8,3,3,512]{4,1,3,2,0:T(8,128)} async-done(((f32[32,8,3,3,512]{4,1,3,2,0:T(8,128)}), f32[1,8,3,3,512]{4,1,3,2,0:T(8,128)}) %reduce-scatter.5.cloned.1.call-update) | async-done | bytes 147472 | tf_op jit(solution)/shard_map/reduce_scatter | solution.py:51
  (96 shorter events, 30.3 us)
Async XLA Ops:
  9.9 56.2 %all-to-all-start = ((f32[64,1,64]{2,1,0:T(1,128)}), f32[64,1,64]{2,1,0:T(1,128)S(1)}, u32[]{:S(2)}, u32[]{:S(2)}) async-start(f32[64,1,64]{2,1,0:T(1,128)} %broadcast_in_dim.10), calls=%async_computation | async-start | bytes 65536 | tf_op jit(solution)/shard_map/all_to_all | solution.py:17
  44.1 82.3 %reduce-scatter.3.cloned.1.call-start = ((), (), s32[]{:S(2)}) async-start(), calls=%async_computation.3 | async-start | bytes 14155776 | tf_op jit(solution)/shard_map/reduce_scatter | solution.py:51
  45.7 24.3 %copy-start.17 = (f32[512]{0:T(512)S(1)}, f32[512]{0:T(512)}, u32[]{:S(2)}) copy-start(f32[512]{0:T(512)} %param.8) | copy-start | bytes 6148
  45.7 24.3 %copy-start.18 = (f32[512]{0:T(512)S(1)}, f32[512]{0:T(512)}, u32[]{:S(2)}) copy-start(f32[512]{0:T(512)} %param.9) | copy-start | bytes 6148
  45.7 20.8 %collective-permute-start = (bf16[1,256,512]{1,2,0:T(8,128)(2,1)S(1)}, bf16[1,256,512]{1,2,0:T(8,128)(2,1)S(1)}, u32[]{:S(2)}, u32[]{:S(2)}) collective-permute-start(bf16[1,256,512]{1,2,0:T(8,128)(2,1)S(1)} %get-tuple-element.22), channel_id=1, source_target_pairs={{0,1},{1,2},{2,3},{3,4},{4,5},{5,6},{6,7},{7,8},{8,9},{9,10},{10,1... | collective-permute-start | bytes 786440 | tf_op jit(solution)/shard_map/ppermute | solution.py:38
  47.0 20.1 %collective-permute-start.1 = (bf16[1,256,512]{1,2,0:T(8,128)(2,1)S(1)}, bf16[1,256,512]{1,2,0:T(8,128)(2,1)}, u32[]{:S(2)}, u32[]{:S(2)}) collective-permute-start(bf16[1,256,512]{1,2,0:T(8,128)(2,1)S(1)} %get-tuple-element.21), channel_id=1, source_target_pairs={{1,0},{2,1},{3,2},{4,3},{5,4},{6,5},{7,6},{8,7},{9,8},{10,9},{11,1... | collective-permute-start | bytes 786440 | tf_op jit(solution)/shard_map/ppermute | solution.py:41
  70.0 3.6 %copy-start = (bf16[4,256,512]{2,1,0:T(8,128)(2,1)S(1)}, bf16[4,256,512]{2,1,0:T(8,128)(2,1)}, u32[]{:S(2)}) copy-start(bf16[4,256,512]{2,1,0:T(8,128)(2,1)} %param.5) | copy-start | bytes 3145732
  78.7 2.3 copy-start.3
  85.2 2.3 copy-start.15
  101.6 169.8 %reduce-scatter.5.cloned.1.call-start = ((), (), s32[]{:S(2)}) async-start(), calls=%async_computation.4 | async-start | bytes 4866048 | tf_op jit(solution)/shard_map/reduce_scatter | solution.py:51
  134.0 2.4 copy-start.13
  136.4 3.7 %copy-start.12 = (bf16[4,256,512]{1,2,0:T(8,128)(2,1)S(1)}, bf16[4,256,512]{1,2,0:T(8,128)(2,1)}, u32[]{:S(2)}) copy-start(bf16[4,256,512]{1,2,0:T(8,128)(2,1)} %get-tuple-element.17) | copy-start | bytes 3145732
  137.7 3.7 %copy-start.11 = (bf16[4,256,512]{1,2,0:T(8,128)(2,1)S(1)}, bf16[4,256,512]{1,2,0:T(8,128)(2,1)}, u32[]{:S(2)}) copy-start(bf16[4,256,512]{1,2,0:T(8,128)(2,1)} %get-tuple-element.18) | copy-start | bytes 3145732
  141.4 2.8 %copy-start.16 = (bf16[1,256,512]{1,2,0:T(8,128)(2,1)S(1)}, bf16[1,256,512]{1,2,0:T(8,128)(2,1)}, u32[]{:S(2)}) copy-start(bf16[1,256,512]{1,2,0:T(8,128)(2,1)} %copy-done.14) | copy-start | bytes 786436
  146.8 4.8 %copy-start.4 = (bf16[4,256,512]{2,1,0:T(8,128)(2,1)S(1)}, bf16[4,256,512]{2,1,0:T(8,128)(2,1)}, u32[]{:S(2)}) copy-start(bf16[4,256,512]{2,1,0:T(8,128)(2,1)} %copy.56) | copy-start | bytes 3145732
  146.8 10.4 %slice-start = ((s8[4718592]{0:T(1024)(128)(4,1)}), s8[524288]{0:T(1024)(128)(4,1)S(1)}, s32[]{:S(2)}) async-start(s8[4718592]{0:T(1024)(128)(4,1)} %bitcast.104), calls=%async_computation.5 | async-start | bytes 1048576
  151.5 1.9 copy-start.5
  151.5 5.6 %slice-start.1 = ((s8[4718592]{0:T(1024)(128)(4,1)}), s8[4194304]{0:T(1024)(128)(4,1)S(1)}, s32[]{:S(2)}) async-start(s8[4718592]{0:T(1024)(128)(4,1)} %bitcast.104), calls=%async_computation.6 | async-start | bytes 8388608
  153.4 1.9 copy-start.6
  155.3 1.9 copy-start.7
  157.9 1.3 copy-start.9
  159.9 1.7 copy-start.2
  224.7 2.3 copy-start.19
  224.7 2.3 copy-start.20
  (4 other events, 4.4 us)
Sparse Core Ops, SparseCore 0:
  101.7 24.6 reduce-scatter.2
  129.5 141.7 reduce-scatter.4
where the time goes:
time: 279 us; the launch traced here: 278 us
  waiting for transfers between devices  86.9 us (31%)
  blocking collectives  60.7 us (22%)
  starting transfers between devices  37 us (13%)
  matrix products  34.6 us (12%)
  local copies, waits for them, and re-layouts  29.5 us (11%)
  other arithmetic  15.1 us (5%)
  between operations  14.4 us (5%)
    reduce_scatter x2, waiting for transfers between devices, own_block(): parts = lax.psum_scatter(parts, axes[k], scatter_dimension=0, tiled=True)  69.1 us
    psum x2, blocking collectives, over_axes(): shard = lax.psum(shard, axis)  60.7 us
    all_to_all x1, starting transfers between devices, copy_for_each(): return lax.all_to_all(copies, axis, split_axis=0, concat_axis=0, tiled=True)  34.2 us
    dot_general x9, matrix products, local(): lax.dot_general(window, flat_act, (((0,), (0,)), ((), ())), preferred_ele...  21.7 us
    slice x9, local copies, waits for them, and re-layouts, local(): padded[2 - tap_row:2 - tap_row + height, 2 - tap_col:2 - tap_col + columns]  19.1 us
    all_to_all x1, waiting for transfers between devices, copy_for_each(): return lax.all_to_all(copies, axis, split_axis=0, concat_axis=0, tiled=True)  17.7 us
    dot_general x9, matrix products, local(): jnp.dot(window, filters[:, tap_row, tap_col, :], preferred_element_type=j...  12.9 us
  transfers between devices with their start and end apart: 5, of which 3 were waited for; matrix products, arithmetic and copies ran while one was open for 14% of the time, Pallas kernels for 0%

commit v1 on v0

v1 whole, which is shorter than its diff:
```python
import functools

import jax
import jax.numpy as jnp
from jax import lax
from jax.experimental import pallas as pl
from jax.experimental.pallas import tpu as pltpu
from jax.sharding import Mesh
from jax.sharding import PartitionSpec as P


GROUPS = 32
CHIPS = "chip"
CORES = "core"
ROWS = ("chip", "core")
PARTS_ROWS = ("parts", "chip", "core")
CORES_PER_CHIP = 2
SEND_SCALE = 1.0 / 128.0

epsilon = 1e-06
f32, bf16, f16 = jnp.float32, jnp.bfloat16, jnp.float16

FAR = (-15, 15)
MIDDLE = (-12, -9, -6, -3, 0, 3, 6, 9, 12)
HUBS = FAR + MIDDLE
SETS = {
    "far": (FAR[0] + 1, FAR[1] + 1, FAR[1] - 1),
    "left": tuple(h + 1 for h in MIDDLE),
    "right": tuple(h - 1 for h in MIDDLE),
    "kept": HUBS + (0,),
}
BLOCK = 3


def swap_cores(x):
    return lax.ppermute(x, CORES, [(0, 1), (1, 0)])


def along(x, step):
    chips = lax.axis_size(CHIPS)
    return lax.ppermute(x, CHIPS, [(i, (i + step) % chips) for i in range(chips)])


def from_all(vector, axes):
    copies = jnp.broadcast_to(vector, (lax.axis_size(axes), *vector.shape))
    return lax.all_to_all(copies, axes, split_axis=0, concat_axis=0, tiled=True)


def with_halo(block):
    count = lax.axis_size(ROWS)
    forward = [(i, i + 1) for i in range(count - 1)]
    backward = [(target, source) for source, target in forward]
    low = lax.ppermute(block[-1:], ROWS, forward)
    high = lax.ppermute(block[:1], ROWS, backward)
    return jnp.concatenate([low, block, high], axis=0)


def expand(values, channels):
    groups = values.shape[0]
    return jnp.broadcast_to(values[:, None], (groups, channels // groups)).reshape(channels)


def group_total(values):
    return values.reshape(GROUPS, -1).sum(axis=1)


def picked_channels(places, channels, core):
    chips = lax.axis_size(CHIPS)
    own = channels // (chips * CORES_PER_CHIP)
    column = jnp.arange(len(places) * own)
    place = jnp.repeat(jnp.array(places), own)
    owner = (lax.axis_index(CHIPS) - place + 2 * chips) % chips
    channel = (owner * CORES_PER_CHIP + core) * own + column % own
    return (jnp.arange(channels)[:, None] == channel[None, :]).astype(bf16)


def window_kernel(pixels, columns, own, *refs):
    *sides, out_ref = refs
    for side, ref in enumerate(sides):
        x = ref[...].astype(f32)
        rows, flat = x.shape
        at = lax.broadcasted_iota(jnp.int32, x.shape, 1) % columns
        shifted = (
            jnp.where(at == columns - 1, 0.0, pltpu.roll(x, flat - 1, 1)),
            x,
            jnp.where(at == 0, 0.0, pltpu.roll(x, 1, 1)),
        )
        for tap_row in range(3):
            lo = (2 - tap_row) * columns
            for tap_col in range(3):
                part = shifted[tap_col][:, lo : lo + pixels].reshape(rows // own, own, pixels)
                out_ref[:, tap_row * 3 + tap_col, :, side * pixels : (side + 1) * pixels] = part.astype(bf16)


def windows_of(sides, start, count, pixels, columns, own):
    flat = sides[0].shape[1]
    first = start // BLOCK
    return pl.pallas_call(
        functools.partial(window_kernel, pixels, columns, own),
        grid=(count // BLOCK,),
        in_specs=[pl.BlockSpec((BLOCK * own, flat), lambda i: (i + first, 0)) for _ in sides],
        out_specs=pl.BlockSpec((BLOCK, 9, own, len(sides) * pixels), lambda i: (i, 0, 0, 0)),
        out_shape=jax.ShapeDtypeStruct((count, 9, own, len(sides) * pixels), bf16),
        cost_estimate=pl.CostEstimate(
            flops=count * 10**7, bytes_accessed=20 * count * own * flat, transcendentals=0
        ),
    )(*sides)


def steps(features, grad_out, filters, norm_gain, norm_bias):
    height, columns, channels = features.shape
    chips = lax.axis_size(CHIPS)
    pixels = height * columns
    all_pixels = pixels * chips * CORES_PER_CHIP
    members = all_pixels * (channels // GROUPS)
    own = channels // (chips * CORES_PER_CHIP)
    core = lax.axis_index(CORES)

    widened = features.astype(f32)
    partial_value = jnp.sum(widened, axis=(0, 1))
    squares = jnp.sum(widened * widened, axis=(0, 1))
    stats = jnp.concatenate([group_total(partial_value), group_total(squares)])
    all_stats = from_all(stats, ROWS)

    extended = with_halo(grad_out)
    partner_features = swap_cores(features)
    flat = extended.reshape(-1, channels)
    places = sum(SETS.values(), ())
    chosen = jnp.concatenate(
        [picked_channels(places, channels, core), picked_channels(places, channels, 1 - core)], axis=1
    )
    rows = lax.dot_general(chosen, flat, (((0,), (1,)), ((), ())), preferred_element_type=f32).astype(bf16)
    half = len(places) * own
    both = (rows[:half], swap_cores(rows[half:]))
    windows, at = {}, 0
    for name, set_places in SETS.items():
        windows[name] = windows_of(both, at, len(set_places), pixels, columns, own)
        at += len(set_places)
    all_stats, windows, partner_features = lax.optimization_barrier((all_stats, windows, partner_features))

    stats = all_stats.sum(axis=0)
    group_mean = stats[:GROUPS] / members
    group_var = stats[GROUPS:] / members - group_mean * group_mean
    inv_std = lax.rsqrt(group_var + epsilon)
    mean_of, std_of = expand(group_mean, channels), expand(inv_std, channels)

    def activated(block):
        normalized = (block.astype(f32) - mean_of) * std_of
        normed = normalized * norm_gain + norm_bias
        return normalized, normed, jax.nn.sigmoid(normed)

    normalized, normed, sigmoid_z = activated(features)
    _, normed_p, sigmoid_p = activated(partner_features)
    act = jnp.concatenate(
        [
            (normed * sigmoid_z).astype(bf16).reshape(-1, channels),
            (normed_p * sigmoid_p).astype(bf16).reshape(-1, channels),
        ],
        axis=0,
    )

    def pieces(name):
        count = len(SETS[name])
        lhs = windows[name].reshape(count * 9 * own, -1)
        out = jnp.dot(lhs, act, preferred_element_type=f32) * SEND_SCALE
        return out.reshape(count, 9, own, channels)

    first = pieces("far").astype(f16)
    first_left = along(first[:2], -1)
    first_right = along(first[2], 1)
    left = along(pieces("left").astype(f16), -1)
    right = along(pieces("right").astype(f16), 1)
    kept = pieces("kept")
    hub = {
        -15: kept[0] + first_left[0].astype(f32),
        15: kept[1] + first_left[1].astype(f32) + first_right.astype(f32),
    }
    far_to_left, far_to_right, extended, filters = lax.optimization_barrier(
        (hub[15].astype(f16), hub[-15].astype(f16), extended, filters)
    )
    far_left = along(far_to_left, -6)
    far_right = along(far_to_right, 6)

    padded = jnp.pad(extended, ((0, 0), (1, 1), (0, 0)))
    grad_act = jnp.zeros((pixels, channels), f32)
    by_tap = filters.reshape(channels, 9, channels).transpose(1, 0, 2)
    for tap_row in range(3):
        for tap_col in range(3):
            window = padded[
                2 - tap_row : 2 - tap_row + height, 2 - tap_col : 2 - tap_col + columns
            ].reshape(-1, channels)
            grad_act = grad_act + jnp.dot(window, by_tap[tap_row * 3 + tap_col], preferred_element_type=f32)

    grad_pre = grad_act.reshape(height, columns, channels) * (
        sigmoid_z * (1.0 + normed * (1.0 - sigmoid_z))
    )
    bias_part = jnp.sum(grad_pre, axis=(0, 1))
    gain_part = jnp.sum(grad_pre * normalized, axis=(0, 1))
    lead = core == 0
    mine = jnp.where(lead, bias_part, gain_part) + swap_cores(jnp.where(lead, gain_part, bias_part))
    left, right, mine = lax.optimization_barrier((left, right, mine))
    every = from_all(mine, CHIPS)
    total = every.sum(axis=0)
    other = swap_cores(total)
    bias_grad, gain_grad = jnp.where(lead, total, other), jnp.where(lead, other, total)
    mean_grad = group_total(norm_gain * bias_grad) / members
    mean_cross = group_total(norm_gain * gain_grad) / members
    grad_in = std_of * (grad_pre * norm_gain - expand(mean_grad, channels) - normalized * expand(mean_cross, channels))
    grad_in = grad_in.astype(bf16)

    for i, h in enumerate(MIDDLE):
        hub[h] = kept[len(FAR) + i] + left[i].astype(f32) + right[i].astype(f32)
    to_left = along(jnp.stack([hub[-6], hub[12], hub[3]], axis=0).astype(f16), -3).astype(f32)
    to_right = along(jnp.stack([hub[6], hub[-12], hub[-3]], axis=0).astype(f16), 3).astype(f32)
    low = hub[-9] + to_left[0] + to_right[1] + far_right.astype(f32)
    high = hub[9] + to_left[1] + to_right[0] + far_left.astype(f32)
    last_left = along(high.astype(f16), -9).astype(f32)
    last_right = along(low.astype(f16), 9).astype(f32)
    near_left, near_right = to_left[2], to_right[2]
    result = hub[0] + near_left + near_right + last_left + last_right
    filter_grad = result.transpose(1, 0, 2).reshape(own, 3, 3, channels) * (1.0 / (SEND_SCALE * all_pixels))
    return (grad_in, filter_grad, gain_grad, bias_grad)


def solution(mesh):
    chips = mesh.shape["rows"] // CORES_PER_CHIP
    torus = Mesh(
        mesh.devices.reshape(mesh.shape["parts"], chips, CORES_PER_CHIP), PARTS_ROWS
    )
    in_specs = (P(PARTS_ROWS, None, None), P(PARTS_ROWS, None, None), P(), P(), P())
    out_specs = (P(PARTS_ROWS, None, None), P(PARTS_ROWS, None, None, None), P("parts"), P("parts"))
    return jax.shard_map(steps, mesh=torus, in_specs=in_specs, out_specs=out_specs, check_vma=False)
```

time: 279 us -> 189 us (0.68)
  blocking collectives: 60.7 us -> 0 us
  starting transfers between devices: 37 us -> 89.6 us
  waiting for transfers between devices: 86.9 us -> 42.6 us
  local copies, waits for them, and re-layouts: 29.5 us -> 9.63 us
  matrix products: 34.6 us -> 15.7 us
  between operations: 14.4 us -> 1.07 us
  Pallas kernels: 0 us -> 12.6 us
    reduce_scatter x2 -> x0, waiting for transfers between devices: 69.1 us -> none  [own_block(): parts = lax.psum_scatter(parts, axes[k], scatter_dimension=0, tiled=True)]
    psum x2 -> x0, blocking collectives: 60.7 us -> none  [over_axes(): shard = lax.psum(shard, axis)]
    ppermute x2 -> x16, starting transfers between devices: 2.63 us -> 39.4 us  [the longest x10 30.8 us: along(): lax.ppermute(x, CHIPS, [(i, (i + step) % chips) for i in range(chips)])]
    ppermute x2 -> x16, waiting for transfers between devices: 0.01 us -> 34.2 us  [the longest x10 33 us: along(): lax.ppermute(x, CHIPS, [(i, (i + step) % chips) for i in range(chips)])]
    dot_general x18 -> x14, matrix products: 34.6 us -> 15.7 us  [the longest x4 7.39 us: pieces(): out = jnp.dot(lhs, act, preferred_element_type=f32) * SEND_SCALE]
    all_to_all x1 -> x2, starting transfers between devices: 34.2 us -> 50.2 us  [from_all(): return lax.all_to_all(copies, axes, split_axis=0, concat_axis=0, tiled=True)]
    slice x10 -> x4, local copies, waits for them, and re-layouts: 19.2 us -> 4.56 us  [the longest x1 2.09 us: steps(): padded[2 - tap_row:2 - tap_row + height, 2 - tap_col:2 - tap_col + columns]]
    pallas_call x0 -> x4, Pallas kernels: none -> 12.6 us  [windows_of(): pl.pallas_call(functools.partial(window_kernel, pixels, columns, own), gr...]
  transfers between devices with their start and end apart: 5 -> 18, of which waited for: 3 -> 8; matrix products, arithmetic and copies ran while one was open for 14% -> 14% of each run, Pallas kernels for 0% -> 7%
where the time goes in v1:
time: 189 us; the launch traced here: 186 us
  starting transfers between devices  89.6 us (47%)
  waiting for transfers between devices  42.6 us (23%)
  matrix products  15.7 us (8%)
  other arithmetic  15.1 us (8%)
  Pallas kernels  12.6 us (7%)
  local copies, waits for them, and re-layouts  9.63 us (5%)
    all_to_all x2, starting transfers between devices, from_all(): return lax.all_to_all(copies, axes, split_axis=0, concat_axis=0, tiled=True)  50.2 us
    ppermute x10, waiting for transfers between devices, along(): lax.ppermute(x, CHIPS, [(i, (i + step) % chips) for i in range(chips)])  33 us
    ppermute x10, starting transfers between devices, along(): lax.ppermute(x, CHIPS, [(i, (i + step) % chips) for i in range(chips)])  30.8 us
    pallas_call x4, Pallas kernels, windows_of(): pl.pallas_call(functools.partial(window_kernel, pixels, columns, own), gr...  12.6 us
    all_to_all x2, waiting for transfers between devices, from_all(): return lax.all_to_all(copies, axes, split_axis=0, concat_axis=0, tiled=True)  8.48 us
    dot_general x4, matrix products, pieces(): out = jnp.dot(lhs, act, preferred_element_type=f32) * SEND_SCALE  7.39 us
    dot_general x9, matrix products, steps(): jnp.dot(window, by_tap[tap_row * 3 + tap_col], preferred_element_type=f32)  6.8 us
    ppermute x4, starting transfers between devices, swap_cores(): return lax.ppermute(x, CORES, [(0, 1), (1, 0)])  4.19 us
  transfers between devices with their start and end apart: 18, of which 8 were waited for; matrix products, arithmetic and copies ran while one was open for 14% of the time, Pallas kernels for 7%

profile of v1, /device:TPU:38, one launch (start us, length us, event | category | flops | bytes accessed | tf_op | source)
XLA Modules:
  0.0 186.3 jit_solution(5545461996421244128)
XLA Ops:
  3.1 3.1 %collective-permute-start = (bf16[1,256,512]{2,1,0:T(8,128)(2,1)S(1)}, bf16[1,256,512]{2,1,0:T(8,128)(2,1)S(1)}, u32[]{:S(2)}, u32[]{:S(2)}) collective-permute-start(bf16[1,256,512]{2,1,0:T(8,128)(2,1)S(1)} %get-tuple-element.61), channel_id=1, source_target_pairs={{0,1},{1,2},{2,3},{3,4},{4,5},{5,6},{6,7},{7,8},{8,9},{9,10},{10,1... | collective-permute-start | bytes 786440 | tf_op jit(solution)/shard_map/ppermute | solution.py:53
  12.1 2.1 %collective-permute-start.2 = (bf16[264,1536]{1,0:T(8,128)(2,1)}, bf16[264,1536]{1,0:T(8,128)(2,1)S(1)}, u32[]{:S(2)}, u32[]{:S(2)}) collective-permute-start(bf16[264,1536]{1,0:T(8,128)(2,1)} %get-tuple-element.49), channel_id=1, source_target_pairs={{0,1},{1,0},{2,3},{3,2},{4,5},{5,4},{6,7},{7,6},{8,9},{9,8},{10,11... | collective-permute-start | bytes 2433032 | tf_op jit(solution)/shard_map/ppermute | solution.py:36
  15.6 36.1 %all-to-all-start = ((f32[64,1,64]{2,1,0:T(1,128)}), f32[64,1,64]{2,1,0:T(1,128)S(1)}, u32[]{:S(2)}, u32[]{:S(2)}) async-start(f32[64,1,64]{2,1,0:T(1,128)} %broadcast_in_dim.16), calls=%async_computation | async-start | bytes 65536 | tf_op jit(solution)/shard_map/all_to_all | solution.py:46
  52.6 2.0 %shard_map.102 = bf16[3,9,8,2048]{3,2,1,0:T(8,128)(2,1)} custom-call(bf16[264,1536]{1,0:T(8,128)(2,1)} %get-tuple-element.50.refs_0_, bf16[264,1536]{1,0:T(8,128)(2,1)} %copy-done.1), custom_call_target="tpu_custom_call" | custom-call | flops 30000000 | bytes 737280 | tf_op jit(solution)/shard_map/pallas_call | solution.py:98
  54.6 3.3 %shard_map.105 = bf16[9,9,8,2048]{3,2,1,0:T(8,128)(2,1)} custom-call(bf16[264,1536]{1,0:T(8,128)(2,1)} %get-tuple-element.50.refs_0_, bf16[264,1536]{1,0:T(8,128)(2,1)} %copy-done.1), custom_call_target="tpu_custom_call" | custom-call | flops 90000000 | bytes 2211840 | tf_op jit(solution)/shard_map/pallas_call | solution.py:98
  57.9 3.3 %shard_map.104 = bf16[9,9,8,2048]{3,2,1,0:T(8,128)(2,1)} custom-call(bf16[264,1536]{1,0:T(8,128)(2,1)} %get-tuple-element.50.refs_0_, bf16[264,1536]{1,0:T(8,128)(2,1)} %copy-done.1), custom_call_target="tpu_custom_call" | custom-call | flops 90000000 | bytes 2211840 | tf_op jit(solution)/shard_map/pallas_call | solution.py:98
  61.2 4.0 %shard_map.103 = bf16[12,9,8,2048]{3,2,1,0:T(8,128)(2,1)} custom-call(bf16[264,1536]{1,0:T(8,128)(2,1)} %get-tuple-element.50.refs_0_, bf16[264,1536]{1,0:T(8,128)(2,1)} %copy-done.1), custom_call_target="tpu_custom_call" | custom-call | flops 120000000 | bytes 2949120 | tf_op jit(solution)/shard_map/pallas_call | solution.py:98
  65.2 8.5 %all-to-all-done = f32[64,1,64]{2,1,0:T(1,128)S(1)} async-done(((f32[64,1,64]{2,1,0:T(1,128)}), f32[64,1,64]{2,1,0:T(1,128)S(1)}, u32[]{:S(2)}, u32[]{:S(2)}) %all-to-all-start) | async-done | bytes 16416 | tf_op jit(solution)/shard_map/all_to_all | solution.py:46
  74.1 2.7 %fusion.12 = (bf16[4,256,512]{2,1,0:T(8,128)(2,1)S(1)}, bf16[4,256,512]{2,1,0:T(8,128)(2,1)S(1)}) fusion(bf16[4,256,512]{2,1,0:T(8,128)(2,1)S(1)} %copy-done, f32[512]{0:T(512)S(1)} %copy-done.13, f32[512]{0:T(512)S(1)} %copy-done.12, f32[512]{0:T(512)S(1)} %sub.65, f32[512]{0:T(512)S(1)} %mul.146, bf16[4,256,512]{2,1,0:T(8,128)(2,1)} %collective-permute-done.3), kind=kLoop, calls=%fused_computation.16 | loop fusion | flops 10485760 | bytes 4202496 | tf_op jit(solution)/shard_map/convert_element_type | solution.py:156
  78.6 2.4 %fusion.20 = f16[648,512]{1,0:T(8,128)(2,1)} fusion(bf16[648,2048]{1,0:T(8,128)(2,1)S(1)} %bitcast.252, bf16[1024,512]{1,0:T(8,128)(2,1)S(1)} %bitcast.258, bf16[1024,512]{1,0:T(8,128)(2,1)S(1)} %bitcast.254), kind=kOutput, calls=%fused_computation.30 | convolution fusion | flops 1363812352 | bytes 5414912 | tf_op jit(solution)/shard_map/dot_general | solution.py:165
  81.0 2.0 %convolution_multiply_fusion = f32[864,512]{1,0:T(8,128)S(1)} fusion(bf16[864,2048]{1,0:T(8,128)(2,1)S(1)} %bitcast.250, bf16[1024,512]{1,0:T(8,128)(2,1)S(1)} %bitcast.259, bf16[1024,512]{1,0:T(8,128)(2,1)S(1)} %bitcast.255), kind=kOutput, calls=%fused_computation.27 | convolution fusion | flops 1816576000 | bytes 7405568 | tf_op jit(solution)/shard_map/dot_general | solution.py:165
  83.8 2.6 %collective-permute-start.4 = (f16[2,9,8,512]{3,2,1,0:T(8,128)(2,1)S(1)}, f16[2,9,8,512]{3,2,1,0:T(8,128)(2,1)S(1)}, u32[]{:S(2)}, u32[]{:S(2)}) collective-permute-start(f16[2,9,8,512]{3,2,1,0:T(8,128)(2,1)S(1)} %bitcast.263), channel_id=1, source_target_pairs={{0,62},{2,0},{4,2},{6,4},{8,6},{10,8},{12,10},{14,12},{16,14},{18,... | collective-permute-start | bytes 442376 | tf_op jit(solution)/shard_map/ppermute | solution.py:41
  86.4 2.4 %fusion.21 = f16[648,512]{1,0:T(8,128)(2,1)} fusion(bf16[648,2048]{1,0:T(8,128)(2,1)S(1)} %bitcast.251, bf16[1024,512]{1,0:T(8,128)(2,1)S(1)} %bitcast.260, bf16[1024,512]{1,0:T(8,128)(2,1)S(1)} %bitcast.256), kind=kOutput, calls=%fused_computation.31 | convolution fusion | flops 1363812352 | bytes 5414912 | tf_op jit(solution)/shard_map/dot_general | solution.py:165
  88.8 2.0 %collective-permute-start.7 = (f16[9,9,8,512]{3,2,1,0:T(8,128)(2,1)}, f16[9,9,8,512]{3,2,1,0:T(8,128)(2,1)S(1)}, u32[]{:S(2)}, u32[]{:S(2)}) collective-permute-start(f16[9,9,8,512]{3,2,1,0:T(8,128)(2,1)} %bitcast.37), channel_id=1, source_target_pairs={{0,2},{2,4},{4,6},{6,8},{8,10},{10,12},{12,14},{14,16},{16,18},{18... | collective-permute-start | bytes 1990664 | tf_op jit(solution)/shard_map/ppermute | solution.py:41
  91.5 2.1 %pad_slice_fusion = (bf16[4,256,512]{2,1,0:T(8,128)(2,1)S(1)}, bf16[4,256,512]{2,1,0:T(8,128)(2,1)S(1)}, bf16[4,256,512]{2,1,0:T(8,128)(2,1)S(1)}, bf16[4,256,51...) fusion(bf16[6,256,512]{2,1,0:T(8,128)(2,1)S(1)} %constant_dynam, ...), kind=kLoop, calls=%fused_computation.37 | loop fusion | bytes 14155776 | tf_op jit(solution)/shard_map/slice | solution.py:189
  107.4 5.0 %collective-permute-start.10 = (f16[3,9,8,512]{3,2,1,0:T(8,128)(2,1)}, f16[3,9,8,512]{3,2,1,0:T(8,128)(2,1)}, u32[]{:S(2)}, u32[]{:S(2)}) collective-permute-start(f16[3,9,8,512]{3,2,1,0:T(8,128)(2,1)} %pad_maximum_fusion.1), channel_id=1, source_target_pairs={{0,58},{2,60},{4,62},{6,0},{8,2},{10,4},{12,6},{14,8},{16,10},{18,... | collective-permute-start | bytes 663560 | tf_op jit(solution)/shard_map/ppermute | solution.py:41
  113.1 14.1 %all-to-all-start.1 = ((f32[32,1,512]{2,1,0:T(1,128)}), f32[32,1,512]{2,1,0:T(1,128)S(1)}, u32[]{:S(2)}, u32[]{:S(2)}) async-start(f32[32,1,512]{2,1,0:T(1,128)} %broadcast_in_dim.21), calls=%async_computation.1 | async-start | bytes 131072 | tf_op jit(solution)/shard_map/all_to_all | solution.py:46
  127.2 8.5 %collective-permute-start.12 = (f16[9,8,512]{2,1,0:T(8,128)(2,1)}, f16[9,8,512]{2,1,0:T(8,128)(2,1)S(1)}, u32[]{:S(2)}, u32[]{:S(2)}) collective-permute-start(f16[9,8,512]{2,1,0:T(8,128)(2,1)} %get-tuple-element.28), channel_id=1, source_target_pairs={{0,52},{2,54},{4,56},{6,58},{8,60},{10,62},{12,0},{14,2},{16,4},{1... | collective-permute-start | bytes 221192 | tf_op jit(solution)/shard_map/ppermute | solution.py:41
  137.9 4.6 %collective-permute-done.12 = f16[9,8,512]{2,1,0:T(8,128)(2,1)S(1)} collective-permute-done((f16[9,8,512]{2,1,0:T(8,128)(2,1)}, f16[9,8,512]{2,1,0:T(8,128)(2,1)S(1)}, u32[]{:S(2)}, u32[]{:S(2)}) %collective-permute-start.12) | collective-permute-done | bytes 73760 | tf_op jit(solution)/shard_map/ppermute | solution.py:41
  142.5 6.8 %collective-permute-done.14 = f16[9,8,512]{2,1,0:T(8,128)(2,1)S(1)} collective-permute-done((f16[9,8,512]{2,1,0:T(8,128)(2,1)S(1)}, f16[9,8,512]{2,1,0:T(8,128)(2,1)S(1)}, u32[]{:S(2)}, u32[]{:S(2)}) %collective-permute-start.14) | collective-permute-done | bytes 73760 | tf_op jit(solution)/shard_map/ppermute | solution.py:41
  150.6 8.5 %collective-permute-start.13 = (f16[9,8,512]{2,1,0:T(8,128)(2,1)S(1)}, f16[9,8,512]{2,1,0:T(8,128)(2,1)S(1)}, u32[]{:S(2)}, u32[]{:S(2)}) collective-permute-start(f16[9,8,512]{2,1,0:T(8,128)(2,1)S(1)} %get-tuple-element.39), channel_id=1, source_target_pairs={{0,46},{2,48},{4,50},{6,52},{8,54},{10,56},{12,58},{14,60},{16,62}... | collective-permute-start | bytes 221192 | tf_op jit(solution)/shard_map/ppermute | solution.py:41
  159.2 3.2 %collective-permute-start.15 = (f16[9,8,512]{2,1,0:T(8,128)(2,1)S(1)}, f16[9,8,512]{2,1,0:T(8,128)(2,1)S(1)}, u32[]{:S(2)}, u32[]{:S(2)}) collective-permute-start(f16[9,8,512]{2,1,0:T(8,128)(2,1)S(1)} %get-tuple-element.40), channel_id=1, source_target_pairs={{0,18},{2,20},{4,22},{6,24},{8,26},{10,28},{12,30},{14,32},{16,34}... | collective-permute-start | bytes 221192 | tf_op jit(solution)/shard_map/ppermute | solution.py:41
  162.6 6.2 %collective-permute-done.13 = f16[9,8,512]{2,1,0:T(8,128)(2,1)S(1)} collective-permute-done((f16[9,8,512]{2,1,0:T(8,128)(2,1)S(1)}, f16[9,8,512]{2,1,0:T(8,128)(2,1)S(1)}, u32[]{:S(2)}, u32[]{:S(2)}) %collective-permute-start.13) | collective-permute-done | bytes 73760 | tf_op jit(solution)/shard_map/ppermute | solution.py:41
  168.8 12.6 %collective-permute-done.15 = f16[9,8,512]{2,1,0:T(8,128)(2,1)S(1)} collective-permute-done((f16[9,8,512]{2,1,0:T(8,128)(2,1)S(1)}, f16[9,8,512]{2,1,0:T(8,128)(2,1)S(1)}, u32[]{:S(2)}, u32[]{:S(2)}) %collective-permute-start.15) | collective-permute-done | bytes 73760 | tf_op jit(solution)/shard_map/ppermute | solution.py:41
  (115 shorter events, 37.0 us)
Async XLA Ops:
  0.6 8.6 %copy-start.5 = (bf16[4,256,512]{2,1,0:T(8,128)(2,1)S(1)}, bf16[4,256,512]{2,1,0:T(8,128)(2,1)}, u32[]{:S(2)}) copy-start(bf16[4,256,512]{2,1,0:T(8,128)(2,1)} %param.8) | copy-start | bytes 3145732
  1.8 7.5 %collective-permute-start.1 = (bf16[1,256,512]{2,1,0:T(8,128)(2,1)S(1)}, bf16[1,256,512]{2,1,0:T(8,128)(2,1)S(1)}, u32[]{:S(2)}, u32[]{:S(2)}) collective-permute-start(bf16[1,256,512]{2,1,0:T(8,128)(2,1)S(1)} %get-tuple-element.60), channel_id=1, source_target_pairs={{1,0},{2,1},{3,2},{4,3},{5,4},{6,5},{7,6},{8,7},{9,8},{10,9},{11,1... | collective-permute-start | bytes 786440 | tf_op jit(solution)/shard_map/ppermute | solution.py:54
  3.1 6.0 %collective-permute-start = (bf16[1,256,512]{2,1,0:T(8,128)(2,1)S(1)}, bf16[1,256,512]{2,1,0:T(8,128)(2,1)S(1)}, u32[]{:S(2)}, u32[]{:S(2)}) collective-permute-start(bf16[1,256,512]{2,1,0:T(8,128)(2,1)S(1)} %get-tuple-element.61), channel_id=1, source_target_pairs={{0,1},{1,2},{2,3},{3,4},{4,5},{5,6},{6,7},{7,8},{8,9},{9,10},{10,1... | collective-permute-start | bytes 786440 | tf_op jit(solution)/shard_map/ppermute | solution.py:53
  6.2 67.5 %collective-permute-start.3 = (bf16[4,256,512]{2,1,0:T(8,128)(2,1)}, bf16[4,256,512]{2,1,0:T(8,128)(2,1)}, u32[]{:S(2)}, u32[]{:S(2)}) collective-permute-start(bf16[4,256,512]{2,1,0:T(8,128)(2,1)} %param.7), channel_id=1, source_target_pairs={{0,1},{1,0},{2,3},{3,2},{4,5},{5,4},{6,7},{7,6},{8,9},{9,8},{10,11... | collective-permute-start | bytes 3145736 | tf_op jit(solution)/shard_map/ppermute | solution.py:36
  12.1 39.6 %collective-permute-start.2 = (bf16[264,1536]{1,0:T(8,128)(2,1)}, bf16[264,1536]{1,0:T(8,128)(2,1)S(1)}, u32[]{:S(2)}, u32[]{:S(2)}) collective-permute-start(bf16[264,1536]{1,0:T(8,128)(2,1)} %get-tuple-element.49), channel_id=1, source_target_pairs={{0,1},{1,0},{2,3},{3,2},{4,5},{5,4},{6,7},{7,6},{8,9},{9,8},{10,11... | collective-permute-start | bytes 2433032 | tf_op jit(solution)/shard_map/ppermute | solution.py:36
  15.6 58.0 %all-to-all-start = ((f32[64,1,64]{2,1,0:T(1,128)}), f32[64,1,64]{2,1,0:T(1,128)S(1)}, u32[]{:S(2)}, u32[]{:S(2)}) async-start(f32[64,1,64]{2,1,0:T(1,128)} %broadcast_in_dim.16), calls=%async_computation | async-start | bytes 65536 | tf_op jit(solution)/shard_map/all_to_all | solution.py:46
  61.1 12.9 %copy-start.12 = (f32[512]{0:T(512)S(1)}, f32[512]{0:T(512)}, u32[]{:S(2)}) copy-start(f32[512]{0:T(512)} %param.10) | copy-start | bytes 6148
  61.2 12.9 %copy-start.13 = (f32[512]{0:T(512)S(1)}, f32[512]{0:T(512)}, u32[]{:S(2)}) copy-start(f32[512]{0:T(512)} %param.11) | copy-start | bytes 6148
  83.0 22.6 %copy-start.8 = (f32[864,512]{1,0:T(8,128)}, f32[864,512]{1,0:T(8,128)S(1)}, u32[]{:S(2)}) copy-start(f32[864,512]{1,0:T(8,128)S(1)} %convolution_multiply_fusion) | copy-start | bytes 5308420
  83.0 7.8 %collective-permute-start.5 = (f16[9,8,512]{2,1,0:T(8,128)(2,1)S(1)}, f16[9,8,512]{2,1,0:T(8,128)(2,1)S(1)}, u32[]{:S(2)}, u32[]{:S(2)}) collective-permute-start(f16[9,8,512]{2,1,0:T(8,128)(2,1)S(1)} %slice_bitcast_fusion.36), channel_id=1, source_target_pairs={{0,2},{2,4},{4,6},{6,8},{8,10},{10,12},{12,14},{14,16},{16,18},{18... | collective-permute-start | bytes 221192 | tf_op jit(solution)/shard_map/ppermute | solution.py:41
  83.8 7.0 %collective-permute-start.4 = (f16[2,9,8,512]{3,2,1,0:T(8,128)(2,1)S(1)}, f16[2,9,8,512]{3,2,1,0:T(8,128)(2,1)S(1)}, u32[]{:S(2)}, u32[]{:S(2)}) collective-permute-start(f16[2,9,8,512]{3,2,1,0:T(8,128)(2,1)S(1)} %bitcast.263), channel_id=1, source_target_pairs={{0,62},{2,0},{4,2},{6,4},{8,6},{10,8},{12,10},{14,12},{16,14},{18,... | collective-permute-start | bytes 442376 | tf_op jit(solution)/shard_map/ppermute | solution.py:41
  88.8 15.7 %collective-permute-start.6 = (f16[9,9,8,512]{3,2,1,0:T(8,128)(2,1)}, f16[9,9,8,512]{3,2,1,0:T(8,128)(2,1)S(1)}, u32[]{:S(2)}, u32[]{:S(2)}) collective-permute-start(f16[9,9,8,512]{3,2,1,0:T(8,128)(2,1)} %bitcast.35), channel_id=1, source_target_pairs={{0,62},{2,0},{4,2},{6,4},{8,6},{10,8},{12,10},{14,12},{16,14},{18,... | collective-permute-start | bytes 1990664 | tf_op jit(solution)/shard_map/ppermute | solution.py:41
  88.8 16.9 %collective-permute-start.7 = (f16[9,9,8,512]{3,2,1,0:T(8,128)(2,1)}, f16[9,9,8,512]{3,2,1,0:T(8,128)(2,1)S(1)}, u32[]{:S(2)}, u32[]{:S(2)}) collective-permute-start(f16[9,9,8,512]{3,2,1,0:T(8,128)(2,1)} %bitcast.37), channel_id=1, source_target_pairs={{0,2},{2,4},{4,6},{6,8},{8,10},{10,12},{12,14},{14,16},{16,18},{18... | collective-permute-start | bytes 1990664 | tf_op jit(solution)/shard_map/ppermute | solution.py:41
  101.6 1.3 collective-permute-start.8
  106.6 29.2 %collective-permute-start.11 = (f16[3,9,8,512]{3,2,1,0:T(8,128)(2,1)S(1)}, f16[3,9,8,512]{3,2,1,0:T(8,128)(2,1)}, u32[]{:S(2)}, u32[]{:S(2)}) collective-permute-start(f16[3,9,8,512]{3,2,1,0:T(8,128)(2,1)S(1)} %pad_maximum_fusion.2), channel_id=1, source_target_pairs={{0,6},{2,8},{4,10},{6,12},{8,14},{10,16},{12,18},{14,20},{16,22},{... | collective-permute-start | bytes 663560 | tf_op jit(solution)/shard_map/ppermute | solution.py:41
  107.4 29.3 %collective-permute-start.10 = (f16[3,9,8,512]{3,2,1,0:T(8,128)(2,1)}, f16[3,9,8,512]{3,2,1,0:T(8,128)(2,1)}, u32[]{:S(2)}, u32[]{:S(2)}) collective-permute-start(f16[3,9,8,512]{3,2,1,0:T(8,128)(2,1)} %pad_maximum_fusion.1), channel_id=1, source_target_pairs={{0,58},{2,60},{4,62},{6,0},{8,2},{10,4},{12,6},{14,8},{16,10},{18,... | collective-permute-start | bytes 663560 | tf_op jit(solution)/shard_map/ppermute | solution.py:41
  113.1 49.3 %all-to-all-start.1 = ((f32[32,1,512]{2,1,0:T(1,128)}), f32[32,1,512]{2,1,0:T(1,128)S(1)}, u32[]{:S(2)}, u32[]{:S(2)}) async-start(f32[32,1,512]{2,1,0:T(1,128)} %broadcast_in_dim.21), calls=%async_computation.1 | async-start | bytes 131072 | tf_op jit(solution)/shard_map/all_to_all | solution.py:46
  127.2 15.3 %collective-permute-start.12 = (f16[9,8,512]{2,1,0:T(8,128)(2,1)}, f16[9,8,512]{2,1,0:T(8,128)(2,1)S(1)}, u32[]{:S(2)}, u32[]{:S(2)}) collective-permute-start(f16[9,8,512]{2,1,0:T(8,128)(2,1)} %get-tuple-element.28), channel_id=1, source_target_pairs={{0,52},{2,54},{4,56},{6,58},{8,60},{10,62},{12,0},{14,2},{16,4},{1... | collective-permute-start | bytes 221192 | tf_op jit(solution)/shard_map/ppermute | solution.py:41
  135.7 13.6 %collective-permute-start.14 = (f16[9,8,512]{2,1,0:T(8,128)(2,1)S(1)}, f16[9,8,512]{2,1,0:T(8,128)(2,1)S(1)}, u32[]{:S(2)}, u32[]{:S(2)}) collective-permute-start(f16[9,8,512]{2,1,0:T(8,128)(2,1)S(1)} %get-tuple-element.29), channel_id=1, source_target_pairs={{0,12},{2,14},{4,16},{6,18},{8,20},{10,22},{12,24},{14,26},{16,28}... | collective-permute-start | bytes 221192 | tf_op jit(solution)/shard_map/ppermute | solution.py:41
  136.7 12.6 %copy-start.6 = (f32[3,9,8,512]{3,2,1,0:T(8,128)}, f32[3,9,8,512]{3,2,1,0:T(8,128)S(1)}, u32[]{:S(2)}) copy-start(f32[3,9,8,512]{3,2,1,0:T(8,128)S(1)} %convert_element_type.205) | copy-start | bytes 1327108
  137.9 12.7 %copy-start.7 = (f32[3,9,8,512]{3,2,1,0:T(8,128)}, f32[3,9,8,512]{3,2,1,0:T(8,128)S(1)}, u32[]{:S(2)}) copy-start(f32[3,9,8,512]{3,2,1,0:T(8,128)S(1)} %convert_element_type.198) | copy-start | bytes 1327108
  150.6 18.2 %collective-permute-start.13 = (f16[9,8,512]{2,1,0:T(8,128)(2,1)S(1)}, f16[9,8,512]{2,1,0:T(8,128)(2,1)S(1)}, u32[]{:S(2)}, u32[]{:S(2)}) collective-permute-start(f16[9,8,512]{2,1,0:T(8,128)(2,1)S(1)} %get-tuple-element.39), channel_id=1, source_target_pairs={{0,46},{2,48},{4,50},{6,52},{8,54},{10,56},{12,58},{14,60},{16,62}... | collective-permute-start | bytes 221192 | tf_op jit(solution)/shard_map/ppermute | solution.py:41
  159.2 22.3 %collective-permute-start.15 = (f16[9,8,512]{2,1,0:T(8,128)(2,1)S(1)}, f16[9,8,512]{2,1,0:T(8,128)(2,1)S(1)}, u32[]{:S(2)}, u32[]{:S(2)}) collective-permute-start(f16[9,8,512]{2,1,0:T(8,128)(2,1)S(1)} %get-tuple-element.40), channel_id=1, source_target_pairs={{0,18},{2,20},{4,22},{6,24},{8,26},{10,28},{12,30},{14,32},{16,34}... | collective-permute-start | bytes 221192 | tf_op jit(solution)/shard_map/ppermute | solution.py:41
  162.5 20.9 %collective-permute-start.9 = (f32[512]{0:T(512)S(1)}, f32[512]{0:T(512)S(1)}, u32[]{:S(2)}, u32[]{:S(2)}) collective-permute-start(f32[512]{0:T(512)S(1)} %reduce_sum.97), channel_id=1, source_target_pairs={{0,1},{1,0},{2,3},{3,2},{4,5},{5,4},{6,7},{7,6},{8,9},{9,8},{10,11... | collective-permute-start | bytes 6152 | tf_op jit(solution)/shard_map/ppermute | solution.py:36
  (10 other events, 28.2 us)

commit v2 on v1

v2 whole, which is shorter than its diff:
```python
import jax
import jax.numpy as jnp
from jax import lax
from jax.sharding import Mesh
from jax.sharding import PartitionSpec as P


GROUPS = 32
CHIPS = "chip"
CORES = "core"
ROWS = ("chip", "core")
PARTS_ROWS = ("parts", "chip", "core")
CORES_PER_CHIP = 2
SEND_SCALE = 1.0 / 128.0
SUM_SCALE = 1.0 / 32768.0
LOW_SCALE = 2048.0

epsilon = 1e-06
f32, bf16, f16 = jnp.float32, jnp.bfloat16, jnp.float16

FAR = (-15, 15)
MIDDLE = (-12, -9, -6, -3, 0, 3, 6, 9, 12)
HUBS = FAR + MIDDLE
SETS = {
    "far": (FAR[0] + 1, FAR[1] + 1, FAR[1] - 1),
    "left": tuple(h + 1 for h in MIDDLE),
    "right": tuple(h - 1 for h in MIDDLE),
    "kept": HUBS,
}


def swap_cores(x):
    return lax.ppermute(x, CORES, [(0, 1), (1, 0)])


def along(x, step):
    chips = lax.axis_size(CHIPS)
    return lax.ppermute(x, CHIPS, [(i, (i + step) % chips) for i in range(chips)])


def from_all(vector, axes):
    copies = jnp.broadcast_to(vector, (lax.axis_size(axes), *vector.shape))
    return lax.all_to_all(copies, axes, split_axis=0, concat_axis=0, tiled=True)


def with_halo(block):
    count = lax.axis_size(ROWS)
    forward = [(i, i + 1) for i in range(count - 1)]
    backward = [(target, source) for source, target in forward]
    low = lax.ppermute(block[-1:], ROWS, forward)
    high = lax.ppermute(block[:1], ROWS, backward)
    return jnp.concatenate([low, block, high], axis=0)


def expand(values, channels):
    groups = values.shape[0]
    return jnp.broadcast_to(values[:, None], (groups, channels // groups)).reshape(channels)


def group_total(values):
    return values.reshape(GROUPS, -1).sum(axis=1)


def picked_channels(places, channels, core):
    chips = lax.axis_size(CHIPS)
    own = channels // (chips * CORES_PER_CHIP)
    column = jnp.arange(len(places) * own)
    place = jnp.repeat(jnp.array(places), own)
    owner = (lax.axis_index(CHIPS) - place + 2 * chips) % chips
    channel = (owner * CORES_PER_CHIP + core) * own + column % own
    return (jnp.arange(channels)[:, None] == channel[None, :]).astype(bf16)


def column_shifts(rows, columns):
    flat = rows.shape[1]
    at = lax.broadcasted_iota(jnp.int32, rows.shape, 1) % columns
    edge = jnp.zeros((rows.shape[0], 1), rows.dtype)
    ahead = jnp.concatenate([rows[:, 1:], edge], axis=1)
    behind = jnp.concatenate([edge, rows[:, : flat - 1]], axis=1)
    zero = jnp.zeros((), rows.dtype)
    return (
        jnp.where(at == columns - 1, zero, ahead),
        rows,
        jnp.where(at == 0, zero, behind),
    )


def coded(sums):
    scaled = sums * SUM_SCALE
    high = scaled.astype(f16)
    low = ((scaled - high.astype(f32)) * LOW_SCALE).astype(f16)
    return jnp.pad(jnp.concatenate([high, low], axis=0), ((0, 8 - 2 * sums.shape[0]), (0, 0)))[None]


def decoded(tile, count):
    wide = tile.astype(f32)
    return (wide[:count] + wide[count : 2 * count] * (1.0 / LOW_SCALE)) * (1.0 / SUM_SCALE)


def send(terms, sums, step):
    own, channels = terms.shape[-2:]
    packed = jnp.concatenate([terms.reshape(-1, own, channels), coded(sums)], axis=0)
    got = along(packed, step)
    return got[:-1].reshape(terms.shape), decoded(got[-1], sums.shape[0])


def steps(features, grad_out, filters, norm_gain, norm_bias):
    height, columns, channels = features.shape
    chips = lax.axis_size(CHIPS)
    pixels = height * columns
    all_pixels = pixels * chips * CORES_PER_CHIP
    members = all_pixels * (channels // GROUPS)
    own = channels // (chips * CORES_PER_CHIP)
    core = lax.axis_index(CORES)

    widened = features.astype(f32)
    partial_value = jnp.sum(widened, axis=(0, 1))
    squares = jnp.sum(widened * widened, axis=(0, 1))
    stats = jnp.concatenate([group_total(partial_value), group_total(squares)])
    all_stats = from_all(stats, ROWS)

    extended = with_halo(grad_out)
    partner_features = swap_cores(features)
    flat = extended.reshape(-1, channels)
    places = sum(SETS.values(), ())
    chosen = jnp.concatenate(
        [picked_channels(places, channels, core), picked_channels(places, channels, 1 - core)], axis=1
    )
    rows = lax.dot_general(chosen, flat, (((0,), (1,)), ((), ())), preferred_element_type=f32).astype(bf16)
    half = len(places) * own
    both = (rows[:half], swap_cores(rows[half:]))
    lines = [b[:, k * columns : (k + 1) * columns] for k in range(height + 2) for b in both]
    shifted = column_shifts(jnp.concatenate(lines, axis=1), columns)
    windows, at = {}, 0
    for name, set_places in SETS.items():
        end = at + len(set_places) * own
        windows[name] = jnp.concatenate([x[at:end] for x in shifted], axis=0)
        at = end
    late_windows = windows.pop("kept")
    padded = jnp.pad(extended, ((0, 0), (1, 1), (0, 0)))
    grad_act = jnp.zeros((pixels, channels), f32)
    by_tap = filters.reshape(channels, 9, channels).transpose(1, 0, 2)
    for tap_row in range(3):
        for tap_col in range(3):
            window = padded[
                2 - tap_row : 2 - tap_row + height, 2 - tap_col : 2 - tap_col + columns
            ].reshape(-1, channels)
            grad_act = grad_act + jnp.dot(window, by_tap[tap_row * 3 + tap_col], preferred_element_type=f32)

    all_stats, grad_act, windows, partner_features = lax.optimization_barrier(
        (all_stats, grad_act, windows, partner_features)
    )

    stats = all_stats.sum(axis=0)
    group_mean = stats[:GROUPS] / members
    group_var = stats[GROUPS:] / members - group_mean * group_mean
    inv_std = lax.rsqrt(group_var + epsilon)
    mean_of, std_of = expand(group_mean, channels), expand(inv_std, channels)

    def activated(block):
        normalized = (block.astype(f32) - mean_of) * std_of
        normed = normalized * norm_gain + norm_bias
        return normalized, normed, jax.nn.sigmoid(normed)

    normalized, normed, sigmoid_z = activated(features)
    _, normed_p, sigmoid_p = activated(partner_features)
    act = jnp.stack([(normed * sigmoid_z).astype(bf16), (normed_p * sigmoid_p).astype(bf16)], axis=1)
    act = act.reshape(-1, channels)

    grad_pre = grad_act.reshape(height, columns, channels) * (
        sigmoid_z * (1.0 + normed * (1.0 - sigmoid_z))
    )
    mine = jnp.stack([jnp.sum(grad_pre, axis=(0, 1)), jnp.sum(grad_pre * normalized, axis=(0, 1))])
    sums = mine + swap_cores(mine)

    def pieces(name, dtype):
        count = len(SETS[name])
        taps = []
        for tap_row in range(3):
            lo = (2 - tap_row) * 2 * columns
            lhs = windows[name][:, lo : lo + act.shape[0]]
            out = (jnp.dot(lhs, act, preferred_element_type=f32) * SEND_SCALE).astype(dtype)
            taps.append(out.reshape(3, count, own, channels))
        return jnp.concatenate(taps, axis=0)

    first = pieces("far", f16)
    first_left, sums_right = send(first[:, :2], sums, -1)
    first_right, sums_left = send(first[:, 2], sums, 1)
    left = along(pieces("left", f16), -1)
    right = along(pieces("right", f16), 1)
    windows["kept"] = late_windows
    kept = pieces("kept", f32)
    hub = {
        -15: kept[:, 0] + first_left[:, 0].astype(f32),
        15: kept[:, 1] + first_left[:, 1].astype(f32) + first_right.astype(f32),
    }
    far_to_left, far_to_right, kept = lax.optimization_barrier(
        (hub[15].astype(f16), hub[-15].astype(f16), kept)
    )
    sums_2 = sums + sums_right
    sums_3 = sums_2 + sums_left
    far_left, next_3 = send(far_to_left, sums_3, -3)
    far_right, last_32 = send(far_to_right, jnp.concatenate([sums_3, sums_2]), 3)
    far_left, far_right, next_3, last_32 = lax.optimization_barrier((far_left, far_right, next_3, last_32))
    sums_9 = sums_3 + next_3 + last_32[:2]
    for i, h in enumerate(MIDDLE):
        hub[h] = kept[:, len(FAR) + i] + left[:, i].astype(f32) + right[:, i].astype(f32)
    hub[12] = hub[12] + far_left.astype(f32)
    hub[-12] = hub[-12] + far_right.astype(f32)
    to_left, next_6 = send(jnp.stack([hub[-6], hub[12]], axis=0).astype(f16), next_3, -3)
    to_right, last_6 = send(jnp.stack([hub[6], hub[-12]], axis=0).astype(f16), last_32[2:], 3)
    near_left = along(hub[3].astype(f16), -3)
    near_right = along(hub[-3].astype(f16), 3)
    to_left, to_right, next_6, last_6 = lax.optimization_barrier((to_left, to_right, next_6, last_6))
    to_left, to_right = to_left.astype(f32), to_right.astype(f32)
    low = hub[-9] + to_left[0] + to_right[1]
    high = hub[9] + to_left[1] + to_right[0]
    last_left, ahead_12 = send(high.astype(f16), sums_9 + next_6, -9)
    last_right, behind_11 = send(low.astype(f16), sums_9 + last_6, 9)
    near = hub[0] + near_left.astype(f32) + near_right.astype(f32)
    bias_grad, gain_grad = sums_9 + ahead_12 + behind_11
    group_of = jnp.arange(channels) // (channels // GROUPS)
    same_group = (group_of[:, None] == group_of[None, :]).astype(f32)
    weighted = jnp.stack([norm_gain * bias_grad, norm_gain * gain_grad])
    mean_grad, mean_cross = jnp.dot(weighted, same_group, precision=lax.Precision.HIGHEST) / members
    grad_in = std_of * (
        grad_pre * norm_gain
        - mean_grad
        - normalized * mean_cross
    )
    result = near + last_left.astype(f32) + last_right.astype(f32)
    filter_grad = result.transpose(1, 0, 2).reshape(own, 3, 3, channels) * (1.0 / (SEND_SCALE * all_pixels))
    return (grad_in.astype(bf16), filter_grad, gain_grad, bias_grad)


def solution(mesh):
    chips = mesh.shape["rows"] // CORES_PER_CHIP
    torus = Mesh(
        mesh.devices.reshape(mesh.shape["parts"], chips, CORES_PER_CHIP), PARTS_ROWS
    )
    in_specs = (P(PARTS_ROWS, None, None), P(PARTS_ROWS, None, None), P(), P(), P())
    out_specs = (P(PARTS_ROWS, None, None), P(PARTS_ROWS, None, None, None), P("parts"), P("parts"))
    return jax.shard_map(steps, mesh=torus, in_specs=in_specs, out_specs=out_specs, check_vma=False)
```

time: 189 us -> 175 us (0.926)
  Pallas kernels: 12.6 us -> 0 us
  starting transfers between devices: 89.6 us -> 83.7 us
  matrix products: 15.7 us -> 18.3 us
  waiting for transfers between devices: 42.6 us -> 44.9 us
    all_to_all x2 -> x1, starting transfers between devices: 50.2 us -> 34.2 us  [from_all(): return lax.all_to_all(copies, axes, split_axis=0, concat_axis=0, tiled=True)]
    pallas_call x4 -> x0, Pallas kernels: 12.6 us -> none  [windows_of(): pl.pallas_call(functools.partial(window_kernel, pixels, columns, own), gr...]
    ppermute x10 -> x12, waiting for transfers between devices: 33 us -> 44.9 us  [along(): lax.ppermute(x, CHIPS, [(i, (i + step) % chips) for i in range(chips)])]
    ppermute x10 -> x12, starting transfers between devices: 30.8 us -> 42.4 us  [along(): lax.ppermute(x, CHIPS, [(i, (i + step) % chips) for i in range(chips)])]
    all_to_all x2 -> x1, waiting for transfers between devices: 8.48 us -> 0.01 us  [from_all(): return lax.all_to_all(copies, axes, split_axis=0, concat_axis=0, tiled=True)]
    convert_element_type x5 -> x23, other arithmetic: 7.71 us -> 2.12 us  [the longest x1 1.62 us: steps(): return (grad_in.astype(bf16), filter_grad, gain_grad, bias_grad)]
    concatenate x0 -> x17, other arithmetic: none -> 3.63 us  [the longest x4 2.53 us: steps(): windows[name] = jnp.concatenate([x[at:end] for x in shifted], axis=0)]
    slice x1 -> x17, local copies, waits for them, and re-layouts: 0.03 us -> 3.36 us  [the longest x9 2.5 us: steps(): windows[name] = jnp.concatenate([x[at:end] for x in shifted], axis=0)]
  transfers between devices with their start and end apart: 18 -> 18, of which waited for: 8 -> 8; matrix products, arithmetic and copies ran while one was open for 14% -> 14% of each run, Pallas kernels for 7% -> 0%
where the time goes in v2:
time: 175 us; the launch traced here: 173 us
  starting transfers between devices  83.7 us (48%)
  waiting for transfers between devices  44.9 us (26%)
  matrix products  18.3 us (10%)
  other arithmetic  14 us (8%)
  local copies, waits for them, and re-layouts  10.7 us (6%)
    ppermute x12, waiting for transfers between devices, along(): lax.ppermute(x, CHIPS, [(i, (i + step) % chips) for i in range(chips)])  44.9 us
    ppermute x12, starting transfers between devices, along(): lax.ppermute(x, CHIPS, [(i, (i + step) % chips) for i in range(chips)])  42.4 us
    all_to_all x1, starting transfers between devices, from_all(): return lax.all_to_all(copies, axes, split_axis=0, concat_axis=0, tiled=True)  34.2 us
    dot_general x9, matrix products, steps(): jnp.dot(window, by_tap[tap_row * 3 + tap_col], preferred_element_type=f32)  9.23 us
    dot_general x12, matrix products, pieces(): jnp.dot(lhs, act, preferred_element_type=f32) * SEND_SCALE  7.55 us
  transfers between devices with their start and end apart: 18, of which 8 were waited for; matrix products, arithmetic and copies ran while one was open for 14% of the time, Pallas kernels for 0%

profile of v2, /device:TPU:38, one launch (start us, length us, event | category | flops | bytes accessed | tf_op | source)
XLA Modules:
  0.0 173.2 jit_solution(16317851165614893032)
XLA Ops:
  0.8 1.6 convert_reduce_fusion
  3.6 34.2 %all-to-all-start = ((f32[64,1,64]{2,1,0:T(1,128)}), f32[64,1,64]{2,1,0:T(1,128)S(1)}, u32[]{:S(2)}, u32[]{:S(2)}) async-start(f32[64,1,64]{2,1,0:T(1,128)} %broadcast_in_dim.29), calls=%async_computation | async-start | bytes 65536 | tf_op jit(solution)/shard_map/all_to_all | solution.py:43
  40.2 3.1 %collective-permute-start = (bf16[1,256,512]{2,1,0:T(8,128)(2,1)S(1)}, bf16[1,256,512]{2,1,0:T(8,128)(2,1)S(1)}, u32[]{:S(2)}, u32[]{:S(2)}) collective-permute-start(bf16[1,256,512]{2,1,0:T(8,128)(2,1)S(1)} %get-tuple-element.81), channel_id=1, source_target_pairs={{0,1},{1,2},{2,3},{3,4},{4,5},{5,6},{6,7},{7,8},{8,9},{9,10},{10,1... | collective-permute-start | bytes 786440 | tf_op jit(solution)/shard_map/ppermute | solution.py:50
  43.5 1.7 %fusion.47 = f32[1024,512]{1,0:T(8,128)S(1)} fusion(bf16[1024,512]{1,0:T(8,128)(2,1)S(1)} %bitcast.237, bf16[9,512,512]{2,1,0:T(8,128)(2,1)} %bitcast.247), kind=kOutput, calls=%fused_computation.89 | convolution fusion | flops 536870912 | bytes 3670016 | tf_op jit(solution)/shard_map/dot_general | solution.py:148
  45.8 1.6 pad_slice_fusion
  53.6 2.5 %collective-permute-start.2 = (bf16[256,1536]{1,0:T(8,128)(2,1)S(1)}, bf16[256,1536]{1,0:T(8,128)(2,1)S(1)}, u32[]{:S(2)}, u32[]{:S(2)}) collective-permute-start(bf16[256,1536]{1,0:T(8,128)(2,1)S(1)} %slice.563), channel_id=1, source_target_pairs={{0,1},{1,0},{2,3},{3,2},{4,5},{5,4},{6,7},{7,6},{8,9},{9,8},{10,11... | collective-permute-start | bytes 2359304 | tf_op jit(solution)/shard_map/ppermute | solution.py:33
  56.0 2.6 %add_add_fusion = f32[1024,512]{1,0:T(8,128)} fusion(f32[1024,512]{1,0:T(8,128)S(1)} %fusion.44, f32[1024,512]{1,0:T(8,128)S(1)} %fusion.45, f32[1024,512]{1,0:T(8,128)S(1)} %fusion.46, f32[1024,512]{1,0:T(8,128)S(1)} %fusion.47, f32[1024,512]{1,0:T(8,128)S(1)} %fusion.48, f32[1024,512]{1,0:T(8,128)S(1)} %fusion.49, f32[1024,512]{1,0:T(8,128)S(1)} %fusion.51, ...), kind=kOutput, calls=%fused_computation.30 | convolution fusion | flops 541065216 | bytes 20447232 | tf_op jit(solution)/shard_map/dot_general | solution.py:148
  65.3 3.4 %fusion.151 = (f32[512]{0:T(512)S(1)}, f32[512]{0:T(512)S(1)}, f32[4,256,512]{2,1,0:T(8,128)S(1)}, bf16[4,1,256,512]{3,2,1,0:T(8,128)(2,1)S(1)}, bf16[4,1,256,512]{3,2,1,0:T(8,128)(2,1)S(1)}) fusion(f32[512]{0:T(512)S(1)} %mul.300, f32[512]{0:T(512)S(1)} %sub.93, bf16[4,256,512]{2,1,0:T(8,128)(2,1)S(1)} %copy-done, f32[512]{0:T(512)S(1)} %copy-done.10, ...), kind=kLoop, calls=%fused_computation.291 | loop fusion | flops 14679040 | bytes 8400896 | tf_op jit(solution)/shard_map/reduce_sum | solution.py:173
  81.2 3.2 %collective-permute-start.10 = (f16[9,9,8,512]{3,2,0,1:T(8,128)(2,1)S(1)}, f16[9,9,8,512]{3,2,0,1:T(8,128)(2,1)S(1)}, u32[]{:S(2)}, u32[]{:S(2)}) collective-permute-start(f16[9,9,8,512]{3,2,0,1:T(8,128)(2,1)S(1)} %copy.36), channel_id=1, source_target_pairs={{0,2},{2,4},{4,6},{6,8},{8,10},{10,12},{12,14},{14,16},{16,18},{18... | collective-permute-start | bytes 1990664 | tf_op jit(solution)/shard_map/ppermute | solution.py:38
  84.8 3.0 %collective-permute-start.9 = (f16[9,9,8,512]{3,2,0,1:T(8,128)(2,1)S(1)}, f16[9,9,8,512]{3,2,0,1:T(8,128)(2,1)S(1)}, u32[]{:S(2)}, u32[]{:S(2)}) collective-permute-start(f16[9,9,8,512]{3,2,0,1:T(8,128)(2,1)S(1)} %copy.35), channel_id=1, source_target_pairs={{0,62},{2,0},{4,2},{6,4},{8,6},{10,8},{12,10},{14,12},{16,14},{18,... | collective-permute-start | bytes 1990664 | tf_op jit(solution)/shard_map/ppermute | solution.py:38
  88.1 3.3 %collective-permute-start.5 = (f16[19,8,512]{2,1,0:T(8,128)(2,1)S(1)}, f16[19,8,512]{2,1,0:T(8,128)(2,1)S(1)}, u32[]{:S(2)}, u32[]{:S(2)}) collective-permute-start(f16[19,8,512]{2,1,0:T(8,128)(2,1)S(1)} %pad_maximum_fusion.11), channel_id=1, source_target_pairs={{0,62},{2,0},{4,2},{6,4},{8,6},{10,8},{12,10},{14,12},{16,14},{18,... | collective-permute-start | bytes 466952 | tf_op jit(solution)/shard_map/ppermute | solution.py:38
  91.4 12.8 %collective-permute-done.6 = f16[10,8,512]{2,1,0:T(8,128)(2,1)S(1)} collective-permute-done((f16[10,8,512]{2,1,0:T(8,128)(2,1)S(1)}, f16[10,8,512]{2,1,0:T(8,128)(2,1)S(1)}, u32[]{:S(2)}, u32[]{:S(2)}) %collective-permute-start.6) | collective-permute-done | bytes 81952 | tf_op jit(solution)/shard_map/ppermute | solution.py:38
  105.7 5.6 %collective-permute-start.7 = (f16[10,8,512]{2,1,0:T(8,128)(2,1)S(1)}, f16[10,8,512]{2,1,0:T(8,128)(2,1)S(1)}, u32[]{:S(2)}, u32[]{:S(2)}) collective-permute-start(f16[10,8,512]{2,1,0:T(8,128)(2,1)S(1)} %pad_maximum_fusion.17), channel_id=1, source_target_pairs={{0,58},{2,60},{4,62},{6,0},{8,2},{10,4},{12,6},{14,8},{16,10},{18,... | collective-permute-start | bytes 245768 | tf_op jit(solution)/shard_map/ppermute | solution.py:38
  112.4 3.1 %collective-permute-done.7 = f16[10,8,512]{2,1,0:T(8,128)(2,1)S(1)} collective-permute-done((f16[10,8,512]{2,1,0:T(8,128)(2,1)S(1)}, f16[10,8,512]{2,1,0:T(8,128)(2,1)S(1)}, u32[]{:S(2)}, u32[]{:S(2)}) %collective-permute-start.7) | collective-permute-done | bytes 81952 | tf_op jit(solution)/shard_map/ppermute | solution.py:38
  115.5 3.5 %collective-permute-done.8 = f16[10,8,512]{2,1,0:T(8,128)(2,1)S(1)} collective-permute-done((f16[10,8,512]{2,1,0:T(8,128)(2,1)S(1)}, f16[10,8,512]{2,1,0:T(8,128)(2,1)S(1)}, u32[]{:S(2)}, u32[]{:S(2)}) %collective-permute-start.8) | collective-permute-done | bytes 81952 | tf_op jit(solution)/shard_map/ppermute | solution.py:38
  119.5 7.7 %collective-permute-start.11 = (f16[19,8,512]{2,1,0:T(8,128)(2,1)S(1)}, f16[19,8,512]{2,1,0:T(8,128)(2,1)S(1)}, u32[]{:S(2)}, u32[]{:S(2)}) collective-permute-start(f16[19,8,512]{2,1,0:T(8,128)(2,1)S(1)} %pad_maximum_fusion.12), channel_id=1, source_target_pairs={{0,58},{2,60},{4,62},{6,0},{8,2},{10,4},{12,6},{14,8},{16,10},{18,... | collective-permute-start | bytes 466952 | tf_op jit(solution)/shard_map/ppermute | solution.py:38
  127.5 5.1 %collective-permute-start.15 = (f16[9,8,512]{2,1,0:T(8,128)(2,1)S(1)}, f16[9,8,512]{2,1,0:T(8,128)(2,1)S(1)}, u32[]{:S(2)}, u32[]{:S(2)}) collective-permute-start(f16[9,8,512]{2,1,0:T(8,128)(2,1)S(1)} %get-tuple-element.56), channel_id=1, source_target_pairs={{0,58},{2,60},{4,62},{6,0},{8,2},{10,4},{12,6},{14,8},{16,10},{18,... | collective-permute-start | bytes 221192 | tf_op jit(solution)/shard_map/ppermute | solution.py:38
  132.6 5.2 %collective-permute-done.11 = f16[19,8,512]{2,1,0:T(8,128)(2,1)S(1)} collective-permute-done((f16[19,8,512]{2,1,0:T(8,128)(2,1)S(1)}, f16[19,8,512]{2,1,0:T(8,128)(2,1)S(1)}, u32[]{:S(2)}, u32[]{:S(2)}) %collective-permute-start.11) | collective-permute-done | bytes 155680 | tf_op jit(solution)/shard_map/ppermute | solution.py:38
  137.8 3.5 %collective-permute-done.12 = f16[19,8,512]{2,1,0:T(8,128)(2,1)S(1)} collective-permute-done((f16[19,8,512]{2,1,0:T(8,128)(2,1)S(1)}, f16[19,8,512]{2,1,0:T(8,128)(2,1)S(1)}, u32[]{:S(2)}, u32[]{:S(2)}) %collective-permute-start.12) | collective-permute-done | bytes 155680 | tf_op jit(solution)/shard_map/ppermute | solution.py:38
  141.7 5.5 %collective-permute-start.14 = (f16[10,8,512]{2,1,0:T(8,128)(2,1)S(1)}, f16[10,8,512]{2,1,0:T(8,128)(2,1)S(1)}, u32[]{:S(2)}, u32[]{:S(2)}) collective-permute-start(f16[10,8,512]{2,1,0:T(8,128)(2,1)S(1)} %pad_maximum_fusion.20), channel_id=1, source_target_pairs={{0,18},{2,20},{4,22},{6,24},{8,26},{10,28},{12,30},{14,32},{16,34}... | collective-permute-start | bytes 245768 | tf_op jit(solution)/shard_map/ppermute | solution.py:38
  147.2 7.6 %collective-permute-start.13 = (f16[10,8,512]{2,1,0:T(8,128)(2,1)S(1)}, f16[10,8,512]{2,1,0:T(8,128)(2,1)S(1)}, u32[]{:S(2)}, u32[]{:S(2)}) collective-permute-start(f16[10,8,512]{2,1,0:T(8,128)(2,1)S(1)} %pad_maximum_fusion.19), channel_id=1, source_target_pairs={{0,46},{2,48},{4,50},{6,52},{8,54},{10,56},{12,58},{14,60},{16,62}... | collective-permute-start | bytes 245768 | tf_op jit(solution)/shard_map/ppermute | solution.py:38
  154.8 5.3 %collective-permute-done.14 = f16[10,8,512]{2,1,0:T(8,128)(2,1)S(1)} collective-permute-done((f16[10,8,512]{2,1,0:T(8,128)(2,1)S(1)}, f16[10,8,512]{2,1,0:T(8,128)(2,1)S(1)}, u32[]{:S(2)}, u32[]{:S(2)}) %collective-permute-start.14) | collective-permute-done | bytes 81952 | tf_op jit(solution)/shard_map/ppermute | solution.py:38
  160.1 10.2 %collective-permute-done.13 = f16[10,8,512]{2,1,0:T(8,128)(2,1)S(1)} collective-permute-done((f16[10,8,512]{2,1,0:T(8,128)(2,1)S(1)}, f16[10,8,512]{2,1,0:T(8,128)(2,1)S(1)}, u32[]{:S(2)}, u32[]{:S(2)}) %collective-permute-start.13) | collective-permute-done | bytes 81952 | tf_op jit(solution)/shard_map/ppermute | solution.py:38
  170.8 1.6 fusion.21
  (188 shorter events, 34.7 us)
Async XLA Ops:
  0.6 42.7 %copy-start.11 = (s32[32]{0:T(128)S(1)}, s32[32]{0:T(128)}, u32[]{:S(2)}) copy-start(s32[32]{0:T(128)} %constant.145) | copy-start | bytes 388
  0.6 42.9 %copy-start.1 = (bf16[4,256,512]{2,1,0:T(8,128)(2,1)S(1)}, bf16[4,256,512]{2,1,0:T(8,128)(2,1)}, u32[]{:S(2)}) copy-start(bf16[4,256,512]{2,1,0:T(8,128)(2,1)} %param.8) | copy-start | bytes 3145732
  0.7 64.2 %collective-permute-start.3 = (bf16[4,256,512]{2,1,0:T(8,128)(2,1)}, bf16[4,256,512]{2,1,0:T(8,128)(2,1)}, u32[]{:S(2)}, u32[]{:S(2)}) collective-permute-start(bf16[4,256,512]{2,1,0:T(8,128)(2,1)} %param.7), channel_id=1, source_target_pairs={{0,1},{1,0},{2,3},{3,2},{4,5},{5,4},{6,7},{7,6},{8,9},{9,8},{10,11... | collective-permute-start | bytes 3145736 | tf_op jit(solution)/shard_map/ppermute | solution.py:33
  3.6 61.3 %all-to-all-start = ((f32[64,1,64]{2,1,0:T(1,128)}), f32[64,1,64]{2,1,0:T(1,128)S(1)}, u32[]{:S(2)}, u32[]{:S(2)}) async-start(f32[64,1,64]{2,1,0:T(1,128)} %broadcast_in_dim.29), calls=%async_computation | async-start | bytes 65536 | tf_op jit(solution)/shard_map/all_to_all | solution.py:43
  38.9 6.6 %collective-permute-start.1 = (bf16[1,256,512]{2,1,0:T(8,128)(2,1)S(1)}, bf16[1,256,512]{2,1,0:T(8,128)(2,1)S(1)}, u32[]{:S(2)}, u32[]{:S(2)}) collective-permute-start(bf16[1,256,512]{2,1,0:T(8,128)(2,1)S(1)} %get-tuple-element.80), channel_id=1, source_target_pairs={{1,0},{2,1},{3,2},{4,3},{5,4},{6,5},{7,6},{8,7},{9,8},{10,9},{11,1... | collective-permute-start | bytes 786440 | tf_op jit(solution)/shard_map/ppermute | solution.py:51
  40.2 5.3 %collective-permute-start = (bf16[1,256,512]{2,1,0:T(8,128)(2,1)S(1)}, bf16[1,256,512]{2,1,0:T(8,128)(2,1)S(1)}, u32[]{:S(2)}, u32[]{:S(2)}) collective-permute-start(bf16[1,256,512]{2,1,0:T(8,128)(2,1)S(1)} %get-tuple-element.81), channel_id=1, source_target_pairs={{0,1},{1,2},{2,3},{3,4},{4,5},{5,6},{6,7},{7,8},{8,9},{9,10},{10,1... | collective-permute-start | bytes 786440 | tf_op jit(solution)/shard_map/ppermute | solution.py:50
  45.8 2.8 %slice-start = ((s8[4718592]{0:T(1024)(128)(4,1)}), s8[4194304]{0:T(1024)(128)(4,1)S(1)}, s32[]{:S(2)}) async-start(s8[4718592]{0:T(1024)(128)(4,1)} %bitcast.248), calls=%async_computation.1 | async-start | bytes 8388608
  45.8 2.8 %slice-start.1 = ((s8[4718592]{0:T(1024)(128)(4,1)}), s8[524288]{0:T(1024)(128)(4,1)S(1)}, s32[]{:S(2)}) async-start(s8[4718592]{0:T(1024)(128)(4,1)} %bitcast.248), calls=%async_computation.2 | async-start | bytes 1048576
  53.6 5.0 %collective-permute-start.2 = (bf16[256,1536]{1,0:T(8,128)(2,1)S(1)}, bf16[256,1536]{1,0:T(8,128)(2,1)S(1)}, u32[]{:S(2)}, u32[]{:S(2)}) collective-permute-start(bf16[256,1536]{1,0:T(8,128)(2,1)S(1)} %slice.563), channel_id=1, source_target_pairs={{0,1},{1,0},{2,3},{3,2},{4,5},{5,4},{6,7},{7,6},{8,9},{9,8},{10,11... | collective-permute-start | bytes 2359304 | tf_op jit(solution)/shard_map/ppermute | solution.py:33
  70.6 10.0 %copy-start.6 = (f16[9,3,8,512]{3,2,1,0:T(8,128)(2,1)}, f16[9,3,8,512]{3,2,1,0:T(8,128)(2,1)S(1)}, u32[]{:S(2)}) copy-start(f16[9,3,8,512]{3,2,1,0:T(8,128)(2,1)S(1)} %pad_maximum_fusion.10) | copy-start | bytes 663556
  80.4 7.4 %collective-permute-start.4 = (f32[2,512]{1,0:T(2,128)S(1)}, f32[2,512]{1,0:T(2,128)S(1)}, u32[]{:S(2)}, u32[]{:S(2)}) collective-permute-start(f32[2,512]{1,0:T(2,128)S(1)} %pad_maximum_fusion.21), channel_id=1, source_target_pairs={{0,1},{1,0},{2,3},{3,2},{4,5},{5,4},{6,7},{7,6},{8,9},{9,8},{10,11... | collective-permute-start | bytes 12296 | tf_op jit(solution)/shard_map/ppermute | solution.py:33
  81.0 7.0 %slice-start.2 = ((f16[9,3,8,512]{3,2,1,0:T(8,128)(2,1)}), f16[9,2,8,512]{3,2,1,0:T(8,128)(2,1)S(1)}, s32[]{:S(2)}) async-start(f16[9,3,8,512]{3,2,1,0:T(8,128)(2,1)} %copy-done.6), calls=%async_computation.3 | async-start | bytes 294912 | tf_op jit(solution)/shard_map/slice | solution.py:187
  81.2 37.9 %collective-permute-start.10 = (f16[9,9,8,512]{3,2,0,1:T(8,128)(2,1)S(1)}, f16[9,9,8,512]{3,2,0,1:T(8,128)(2,1)S(1)}, u32[]{:S(2)}, u32[]{:S(2)}) collective-permute-start(f16[9,9,8,512]{3,2,0,1:T(8,128)(2,1)S(1)} %copy.36), channel_id=1, source_target_pairs={{0,2},{2,4},{4,6},{6,8},{8,10},{10,12},{12,14},{14,16},{16,18},{18... | collective-permute-start | bytes 1990664 | tf_op jit(solution)/shard_map/ppermute | solution.py:38
  84.8 34.3 %collective-permute-start.9 = (f16[9,9,8,512]{3,2,0,1:T(8,128)(2,1)S(1)}, f16[9,9,8,512]{3,2,0,1:T(8,128)(2,1)S(1)}, u32[]{:S(2)}, u32[]{:S(2)}) collective-permute-start(f16[9,9,8,512]{3,2,0,1:T(8,128)(2,1)S(1)} %copy.35), channel_id=1, source_target_pairs={{0,62},{2,0},{4,2},{6,4},{8,6},{10,8},{12,10},{14,12},{16,14},{18,... | collective-permute-start | bytes 1990664 | tf_op jit(solution)/shard_map/ppermute | solution.py:38
  87.9 16.3 %collective-permute-start.6 = (f16[10,8,512]{2,1,0:T(8,128)(2,1)S(1)}, f16[10,8,512]{2,1,0:T(8,128)(2,1)S(1)}, u32[]{:S(2)}, u32[]{:S(2)}) collective-permute-start(f16[10,8,512]{2,1,0:T(8,128)(2,1)S(1)} %pad_maximum_fusion.16), channel_id=1, source_target_pairs={{0,2},{2,4},{4,6},{6,8},{8,10},{10,12},{12,14},{14,16},{16,18},{18... | collective-permute-start | bytes 245768 | tf_op jit(solution)/shard_map/ppermute | solution.py:38
  88.1 17.4 %collective-permute-start.5 = (f16[19,8,512]{2,1,0:T(8,128)(2,1)S(1)}, f16[19,8,512]{2,1,0:T(8,128)(2,1)S(1)}, u32[]{:S(2)}, u32[]{:S(2)}) collective-permute-start(f16[19,8,512]{2,1,0:T(8,128)(2,1)S(1)} %pad_maximum_fusion.11), channel_id=1, source_target_pairs={{0,62},{2,0},{4,2},{6,4},{8,6},{10,8},{12,10},{14,12},{16,14},{18,... | collective-permute-start | bytes 466952 | tf_op jit(solution)/shard_map/ppermute | solution.py:38
  105.7 9.7 %collective-permute-start.7 = (f16[10,8,512]{2,1,0:T(8,128)(2,1)S(1)}, f16[10,8,512]{2,1,0:T(8,128)(2,1)S(1)}, u32[]{:S(2)}, u32[]{:S(2)}) collective-permute-start(f16[10,8,512]{2,1,0:T(8,128)(2,1)S(1)} %pad_maximum_fusion.17), channel_id=1, source_target_pairs={{0,58},{2,60},{4,62},{6,0},{8,2},{10,4},{12,6},{14,8},{16,10},{18,... | collective-permute-start | bytes 245768 | tf_op jit(solution)/shard_map/ppermute | solution.py:38
  111.4 7.6 %collective-permute-start.8 = (f16[10,8,512]{2,1,0:T(8,128)(2,1)S(1)}, f16[10,8,512]{2,1,0:T(8,128)(2,1)S(1)}, u32[]{:S(2)}, u32[]{:S(2)}) collective-permute-start(f16[10,8,512]{2,1,0:T(8,128)(2,1)S(1)} %pad_maximum_fusion.18), channel_id=1, source_target_pairs={{0,6},{2,8},{4,10},{6,12},{8,14},{10,16},{12,18},{14,20},{16,22},{... | collective-permute-start | bytes 245768 | tf_op jit(solution)/shard_map/ppermute | solution.py:38
  119.5 18.3 %collective-permute-start.11 = (f16[19,8,512]{2,1,0:T(8,128)(2,1)S(1)}, f16[19,8,512]{2,1,0:T(8,128)(2,1)S(1)}, u32[]{:S(2)}, u32[]{:S(2)}) collective-permute-start(f16[19,8,512]{2,1,0:T(8,128)(2,1)S(1)} %pad_maximum_fusion.12), channel_id=1, source_target_pairs={{0,58},{2,60},{4,62},{6,0},{8,2},{10,4},{12,6},{14,8},{16,10},{18,... | collective-permute-start | bytes 466952 | tf_op jit(solution)/shard_map/ppermute | solution.py:38
  127.2 14.1 %collective-permute-start.12 = (f16[19,8,512]{2,1,0:T(8,128)(2,1)S(1)}, f16[19,8,512]{2,1,0:T(8,128)(2,1)S(1)}, u32[]{:S(2)}, u32[]{:S(2)}) collective-permute-start(f16[19,8,512]{2,1,0:T(8,128)(2,1)S(1)} %pad_maximum_fusion.13), channel_id=1, source_target_pairs={{0,6},{2,8},{4,10},{6,12},{8,14},{10,16},{12,18},{14,20},{16,22},{... | collective-permute-start | bytes 466952 | tf_op jit(solution)/shard_map/ppermute | solution.py:38
  127.4 45.1 %collective-permute-start.16 = (f16[9,8,512]{2,1,0:T(8,128)(2,1)S(1)}, f16[9,8,512]{2,1,0:T(8,128)(2,1)S(1)}, u32[]{:S(2)}, u32[]{:S(2)}) collective-permute-start(f16[9,8,512]{2,1,0:T(8,128)(2,1)S(1)} %get-tuple-element.57), channel_id=1, source_target_pairs={{0,6},{2,8},{4,10},{6,12},{8,14},{10,16},{12,18},{14,20},{16,22},{... | collective-permute-start | bytes 221192 | tf_op jit(solution)/shard_map/ppermute | solution.py:38
  127.5 44.9 %collective-permute-start.15 = (f16[9,8,512]{2,1,0:T(8,128)(2,1)S(1)}, f16[9,8,512]{2,1,0:T(8,128)(2,1)S(1)}, u32[]{:S(2)}, u32[]{:S(2)}) collective-permute-start(f16[9,8,512]{2,1,0:T(8,128)(2,1)S(1)} %get-tuple-element.56), channel_id=1, source_target_pairs={{0,58},{2,60},{4,62},{6,0},{8,2},{10,4},{12,6},{14,8},{16,10},{18,... | collective-permute-start | bytes 221192 | tf_op jit(solution)/shard_map/ppermute | solution.py:38
  141.7 18.4 %collective-permute-start.14 = (f16[10,8,512]{2,1,0:T(8,128)(2,1)S(1)}, f16[10,8,512]{2,1,0:T(8,128)(2,1)S(1)}, u32[]{:S(2)}, u32[]{:S(2)}) collective-permute-start(f16[10,8,512]{2,1,0:T(8,128)(2,1)S(1)} %pad_maximum_fusion.20), channel_id=1, source_target_pairs={{0,18},{2,20},{4,22},{6,24},{8,26},{10,28},{12,30},{14,32},{16,34}... | collective-permute-start | bytes 245768 | tf_op jit(solution)/shard_map/ppermute | solution.py:38
  147.2 23.0 %collective-permute-start.13 = (f16[10,8,512]{2,1,0:T(8,128)(2,1)S(1)}, f16[10,8,512]{2,1,0:T(8,128)(2,1)S(1)}, u32[]{:S(2)}, u32[]{:S(2)}) collective-permute-start(f16[10,8,512]{2,1,0:T(8,128)(2,1)S(1)} %pad_maximum_fusion.19), channel_id=1, source_target_pairs={{0,46},{2,48},{4,50},{6,52},{8,54},{10,56},{12,58},{14,60},{16,62}... | collective-permute-start | bytes 245768 | tf_op jit(solution)/shard_map/ppermute | solution.py:38
  (9 other events, 14.9 us)

commit v3 on v2

--- a/solution.py
+++ b/solution.py
@@ -87,9 +87,9 @@
 
 def coded(sums):
     scaled = sums * SUM_SCALE
-    high = scaled.astype(f16)
-    low = ((scaled - high.astype(f32)) * LOW_SCALE).astype(f16)
-    return jnp.pad(jnp.concatenate([high, low], axis=0), ((0, 8 - 2 * sums.shape[0]), (0, 0)))[None]
+    high = lax.reduce_precision(scaled, exponent_bits=5, mantissa_bits=10)
+    low = (scaled - high) * LOW_SCALE
+    return jnp.pad(jnp.concatenate([high, low], axis=0), ((0, 8 - 2 * sums.shape[0]), (0, 0))).astype(f16)[None]
 
 
 def decoded(tile, count):
@@ -136,7 +136,6 @@
         end = at + len(set_places) * own
         windows[name] = jnp.concatenate([x[at:end] for x in shifted], axis=0)
         at = end
-    late_windows = windows.pop("kept")
     padded = jnp.pad(extended, ((0, 0), (1, 1), (0, 0)))
     grad_act = jnp.zeros((pixels, channels), f32)
     by_tap = filters.reshape(channels, 9, channels).transpose(1, 0, 2)
@@ -188,7 +187,6 @@
     first_right, sums_left = send(first[:, 2], sums, 1)
     left = along(pieces("left", f16), -1)
     right = along(pieces("right", f16), 1)
-    windows["kept"] = late_windows
     kept = pieces("kept", f32)
     hub = {
         -15: kept[:, 0] + first_left[:, 0].astype(f32),
@@ -207,17 +205,15 @@
         hub[h] = kept[:, len(FAR) + i] + left[:, i].astype(f32) + right[:, i].astype(f32)
     hub[12] = hub[12] + far_left.astype(f32)
     hub[-12] = hub[-12] + far_right.astype(f32)
-    to_left, next_6 = send(jnp.stack([hub[-6], hub[12]], axis=0).astype(f16), next_3, -3)
-    to_right, last_6 = send(jnp.stack([hub[6], hub[-12]], axis=0).astype(f16), last_32[2:], 3)
-    near_left = along(hub[3].astype(f16), -3)
-    near_right = along(hub[-3].astype(f16), 3)
+    to_left, next_6 = send(jnp.stack([hub[-6], hub[12], hub[3]], axis=0).astype(f16), next_3, -3)
+    to_right, last_6 = send(jnp.stack([hub[6], hub[-12], hub[-3]], axis=0).astype(f16), last_32[2:], 3)
     to_left, to_right, next_6, last_6 = lax.optimization_barrier((to_left, to_right, next_6, last_6))
     to_left, to_right = to_left.astype(f32), to_right.astype(f32)
     low = hub[-9] + to_left[0] + to_right[1]
     high = hub[9] + to_left[1] + to_right[0]
     last_left, ahead_12 = send(high.astype(f16), sums_9 + next_6, -9)
     last_right, behind_11 = send(low.astype(f16), sums_9 + last_6, 9)
-    near = hub[0] + near_left.astype(f32) + near_right.astype(f32)
+    near = hub[0] + to_left[2] + to_right[2]
     bias_grad, gain_grad = sums_9 + ahead_12 + behind_11
     group_of = jnp.arange(channels) // (channels // GROUPS)
     same_group = (group_of[:, None] == group_of[None, :]).astype(f32)

time: 175 us -> 177 us (1.011)
  waiting for transfers between devices: 44.9 us -> 55.1 us
  starting transfers between devices: 83.7 us -> 78.5 us
  local copies, waits for them, and re-layouts: 10.7 us -> 8.76 us
    ppermute x12 -> x10, waiting for transfers between devices: 44.9 us -> 54.4 us  [along(): lax.ppermute(x, CHIPS, [(i, (i + step) % chips) for i in range(chips)])]
    ppermute x12 -> x10, starting transfers between devices: 42.4 us -> 36.8 us  [along(): lax.ppermute(x, CHIPS, [(i, (i + step) % chips) for i in range(chips)])]
    slice x9, local copies, waits for them, and re-layouts: 2.5 us -> 0.32 us  [steps(): windows[name] = jnp.concatenate([x[at:end] for x in shifted], axis=0)]
    concatenate x4, other arithmetic: 2.53 us -> 4.41 us  [steps(): windows[name] = jnp.concatenate([x[at:end] for x in shifted], axis=0)]
  transfers between devices with their start and end apart: 18 -> 16, of which waited for: 8 -> 9; matrix products, arithmetic and copies ran while one was open for 14% -> 13% of each run, Pallas kernels for 0% -> 0%
where the time goes in v3:
time: 177 us; the launch traced here: 176 us
  starting transfers between devices  78.5 us (44%)
  waiting for transfers between devices  55.1 us (31%)
  matrix products  16.7 us (9%)
  other arithmetic  15.6 us (9%)
  local copies, waits for them, and re-layouts  8.76 us (5%)
    ppermute x10, waiting for transfers between devices, along(): lax.ppermute(x, CHIPS, [(i, (i + step) % chips) for i in range(chips)])  54.4 us
    ppermute x10, starting transfers between devices, along(): lax.ppermute(x, CHIPS, [(i, (i + step) % chips) for i in range(chips)])  36.8 us
    all_to_all x1, starting transfers between devices, from_all(): return lax.all_to_all(copies, axes, split_axis=0, concat_axis=0, tiled=True)  34.2 us
    dot_general x9, matrix products, steps(): jnp.dot(window, by_tap[tap_row * 3 + tap_col], preferred_element_type=f32)  7.83 us
    dot_general x12, matrix products, pieces(): jnp.dot(lhs, act, preferred_element_type=f32) * SEND_SCALE  7.37 us
    concatenate x4, other arithmetic, steps(): windows[name] = jnp.concatenate([x[at:end] for x in shifted], axis=0)  4.41 us
  transfers between devices with their start and end apart: 16, of which 9 were waited for; matrix products, arithmetic and copies ran while one was open for 13% of the time, Pallas kernels for 0%

profile of v3, /device:TPU:38, one launch (start us, length us, event | category | flops | bytes accessed | tf_op | source)
XLA Modules:
  0.0 176.3 jit_solution(18164184929016342030)
XLA Ops:
  0.8 1.6 convert_reduce_fusion
  3.6 34.2 %all-to-all-start = ((f32[64,1,64]{2,1,0:T(1,128)}), f32[64,1,64]{2,1,0:T(1,128)S(1)}, u32[]{:S(2)}, u32[]{:S(2)}) async-start(f32[64,1,64]{2,1,0:T(1,128)} %broadcast_in_dim.27), calls=%async_computation | async-start | bytes 65536 | tf_op jit(solution)/shard_map/all_to_all | solution.py:43
  38.9 1.3 collective-permute-start.1
  40.2 3.1 %collective-permute-start = (bf16[1,256,512]{2,1,0:T(8,128)(2,1)S(1)}, bf16[1,256,512]{2,1,0:T(8,128)(2,1)S(1)}, u32[]{:S(2)}, u32[]{:S(2)}) collective-permute-start(bf16[1,256,512]{2,1,0:T(8,128)(2,1)S(1)} %get-tuple-element.81), channel_id=1, source_target_pairs={{0,1},{1,2},{2,3},{3,4},{4,5},{5,6},{6,7},{7,8},{8,9},{9,10},{10,1... | collective-permute-start | bytes 786440 | tf_op jit(solution)/shard_map/ppermute | solution.py:50
  43.5 1.7 fusion.47
  45.8 1.6 pad_slice_fusion
  53.6 2.4 %collective-permute-start.2 = (bf16[256,1536]{1,0:T(8,128)(2,1)S(1)}, bf16[256,1536]{1,0:T(8,128)(2,1)S(1)}, u32[]{:S(2)}, u32[]{:S(2)}) collective-permute-start(bf16[256,1536]{1,0:T(8,128)(2,1)S(1)} %slice.571), channel_id=1, source_target_pairs={{0,1},{1,0},{2,3},{3,2},{4,5},{5,4},{6,7},{7,6},{8,9},{9,8},{10,11... | collective-permute-start | bytes 2359304 | tf_op jit(solution)/shard_map/ppermute | solution.py:33
  65.3 3.1 %fusion.164 = (f32[512]{0:T(512)S(1)}, f32[512]{0:T(512)S(1)}, f32[4,256,512]{2,1,0:T(8,128)S(1)}, bf16[4,1,256,512]{3,2,1,0:T(8,128)(2,1)S(1)}, bf16[4,1,256,512]{3,2,1,0:T(8,128)(2,1)S(1)}) fusion(f32[512]{0:T(512)S(1)} %mul.318, f32[512]{0:T(512)S(1)} %sub.99, bf16[4,256,512]{2,1,0:T(8,128)(2,1)S(1)} %copy-done, f32[512]{0:T(512)S(1)} %copy-done.10, ...), kind=kLoop, calls=%fused_computation.308 | loop fusion | flops 14679040 | bytes 8400896 | tf_op jit(solution)/shard_map/reduce_sum | solution.py:172
  80.3 2.9 %collective-permute-start.10 = (f16[9,9,8,512]{3,2,0,1:T(8,128)(2,1)S(1)}, f16[9,9,8,512]{3,2,0,1:T(8,128)(2,1)S(1)}, u32[]{:S(2)}, u32[]{:S(2)}) collective-permute-start(f16[9,9,8,512]{3,2,0,1:T(8,128)(2,1)S(1)} %copy.36), channel_id=1, source_target_pairs={{0,2},{2,4},{4,6},{6,8},{8,10},{10,12},{12,14},{14,16},{16,18},{18... | collective-permute-start | bytes 1990664 | tf_op jit(solution)/shard_map/ppermute | solution.py:38
  83.5 3.0 %collective-permute-start.9 = (f16[9,9,8,512]{3,2,0,1:T(8,128)(2,1)S(1)}, f16[9,9,8,512]{3,2,0,1:T(8,128)(2,1)S(1)}, u32[]{:S(2)}, u32[]{:S(2)}) collective-permute-start(f16[9,9,8,512]{3,2,0,1:T(8,128)(2,1)S(1)} %copy.35), channel_id=1, source_target_pairs={{0,62},{2,0},{4,2},{6,4},{8,6},{10,8},{12,10},{14,12},{16,14},{18,... | collective-permute-start | bytes 1990664 | tf_op jit(solution)/shard_map/ppermute | solution.py:38
  86.8 3.3 %collective-permute-start.5 = (f16[19,8,512]{2,1,0:T(8,128)(2,1)S(1)}, f16[19,8,512]{2,1,0:T(8,128)(2,1)S(1)}, u32[]{:S(2)}, u32[]{:S(2)}) collective-permute-start(f16[19,8,512]{2,1,0:T(8,128)(2,1)S(1)} %pad_maximum_fusion.15), channel_id=1, source_target_pairs={{0,62},{2,0},{4,2},{6,4},{8,6},{10,8},{12,10},{14,12},{16,14},{18,... | collective-permute-start | bytes 466952 | tf_op jit(solution)/shard_map/ppermute | solution.py:38
  90.2 13.1 %collective-permute-done.6 = f16[10,8,512]{2,1,0:T(8,128)(2,1)S(1)} collective-permute-done((f16[10,8,512]{2,1,0:T(8,128)(2,1)S(1)}, f16[10,8,512]{2,1,0:T(8,128)(2,1)S(1)}, u32[]{:S(2)}, u32[]{:S(2)}) %collective-permute-start.6) | collective-permute-done | bytes 81952 | tf_op jit(solution)/shard_map/ppermute | solution.py:38
  103.3 1.3 collective-permute-done.5
  104.8 5.6 %collective-permute-start.7 = (f16[10,8,512]{2,1,0:T(8,128)(2,1)S(1)}, f16[10,8,512]{2,1,0:T(8,128)(2,1)S(1)}, u32[]{:S(2)}, u32[]{:S(2)}) collective-permute-start(f16[10,8,512]{2,1,0:T(8,128)(2,1)S(1)} %pad_maximum_fusion.17), channel_id=1, source_target_pairs={{0,58},{2,60},{4,62},{6,0},{8,2},{10,4},{12,6},{14,8},{16,10},{18,... | collective-permute-start | bytes 245768 | tf_op jit(solution)/shard_map/ppermute | solution.py:38
  111.2 3.5 %collective-permute-done.7 = f16[10,8,512]{2,1,0:T(8,128)(2,1)S(1)} collective-permute-done((f16[10,8,512]{2,1,0:T(8,128)(2,1)S(1)}, f16[10,8,512]{2,1,0:T(8,128)(2,1)S(1)}, u32[]{:S(2)}, u32[]{:S(2)}) %collective-permute-start.7) | collective-permute-done | bytes 81952 | tf_op jit(solution)/shard_map/ppermute | solution.py:38
  114.7 3.4 %collective-permute-done.8 = f16[10,8,512]{2,1,0:T(8,128)(2,1)S(1)} collective-permute-done((f16[10,8,512]{2,1,0:T(8,128)(2,1)S(1)}, f16[10,8,512]{2,1,0:T(8,128)(2,1)S(1)}, u32[]{:S(2)}, u32[]{:S(2)}) %collective-permute-start.8) | collective-permute-done | bytes 81952 | tf_op jit(solution)/shard_map/ppermute | solution.py:38
  118.7 7.9 %collective-permute-start.11 = (f16[28,8,512]{2,1,0:T(8,128)(2,1)S(1)}, f16[28,8,512]{2,1,0:T(8,128)(2,1)S(1)}, u32[]{:S(2)}, u32[]{:S(2)}) collective-permute-start(f16[28,8,512]{2,1,0:T(8,128)(2,1)S(1)} %pad_maximum_fusion.10), channel_id=1, source_target_pairs={{0,58},{2,60},{4,62},{6,0},{8,2},{10,4},{12,6},{14,8},{16,10},{18,... | collective-permute-start | bytes 688136 | tf_op jit(solution)/shard_map/ppermute | solution.py:38
  126.9 11.6 %collective-permute-done.11 = f16[28,8,512]{2,1,0:T(8,128)(2,1)S(1)} collective-permute-done((f16[28,8,512]{2,1,0:T(8,128)(2,1)S(1)}, f16[28,8,512]{2,1,0:T(8,128)(2,1)S(1)}, u32[]{:S(2)}, u32[]{:S(2)}) %collective-permute-start.11) | collective-permute-done | bytes 229408 | tf_op jit(solution)/shard_map/ppermute | solution.py:38
  138.5 6.0 %collective-permute-done.12 = f16[28,8,512]{2,1,0:T(8,128)(2,1)S(1)} collective-permute-done((f16[28,8,512]{2,1,0:T(8,128)(2,1)S(1)}, f16[28,8,512]{2,1,0:T(8,128)(2,1)S(1)}, u32[]{:S(2)}, u32[]{:S(2)}) %collective-permute-start.12) | collective-permute-done | bytes 229408 | tf_op jit(solution)/shard_map/ppermute | solution.py:38
  144.9 4.1 %collective-permute-start.14 = (f16[10,8,512]{2,1,0:T(8,128)(2,1)S(1)}, f16[10,8,512]{2,1,0:T(8,128)(2,1)S(1)}, u32[]{:S(2)}, u32[]{:S(2)}) collective-permute-start(f16[10,8,512]{2,1,0:T(8,128)(2,1)S(1)} %pad_maximum_fusion.19), channel_id=1, source_target_pairs={{0,18},{2,20},{4,22},{6,24},{8,26},{10,28},{12,30},{14,32},{16,34}... | collective-permute-start | bytes 245768 | tf_op jit(solution)/shard_map/ppermute | solution.py:38
  149.1 9.0 %collective-permute-start.13 = (f16[10,8,512]{2,1,0:T(8,128)(2,1)S(1)}, f16[10,8,512]{2,1,0:T(8,128)(2,1)S(1)}, u32[]{:S(2)}, u32[]{:S(2)}) collective-permute-start(f16[10,8,512]{2,1,0:T(8,128)(2,1)S(1)} %pad_maximum_fusion.18), channel_id=1, source_target_pairs={{0,46},{2,48},{4,50},{6,52},{8,54},{10,56},{12,58},{14,60},{16,62}... | collective-permute-start | bytes 245768 | tf_op jit(solution)/shard_map/ppermute | solution.py:38
  158.1 7.3 %collective-permute-done.14 = f16[10,8,512]{2,1,0:T(8,128)(2,1)S(1)} collective-permute-done((f16[10,8,512]{2,1,0:T(8,128)(2,1)S(1)}, f16[10,8,512]{2,1,0:T(8,128)(2,1)S(1)}, u32[]{:S(2)}, u32[]{:S(2)}) %collective-permute-start.14) | collective-permute-done | bytes 81952 | tf_op jit(solution)/shard_map/ppermute | solution.py:38
  165.4 8.1 %collective-permute-done.13 = f16[10,8,512]{2,1,0:T(8,128)(2,1)S(1)} collective-permute-done((f16[10,8,512]{2,1,0:T(8,128)(2,1)S(1)}, f16[10,8,512]{2,1,0:T(8,128)(2,1)S(1)}, u32[]{:S(2)}, u32[]{:S(2)}) %collective-permute-start.13) | collective-permute-done | bytes 81952 | tf_op jit(solution)/shard_map/ppermute | solution.py:38
  174.0 1.6 fusion.21
  (183 shorter events, 33.7 us)
Async XLA Ops:
  0.6 42.7 %copy-start.11 = (s32[32]{0:T(128)S(1)}, s32[32]{0:T(128)}, u32[]{:S(2)}) copy-start(s32[32]{0:T(128)} %constant.146) | copy-start | bytes 388
  0.6 42.9 %copy-start.1 = (bf16[4,256,512]{2,1,0:T(8,128)(2,1)S(1)}, bf16[4,256,512]{2,1,0:T(8,128)(2,1)}, u32[]{:S(2)}) copy-start(bf16[4,256,512]{2,1,0:T(8,128)(2,1)} %param.8) | copy-start | bytes 3145732
  0.7 64.2 %collective-permute-start.3 = (bf16[4,256,512]{2,1,0:T(8,128)(2,1)}, bf16[4,256,512]{2,1,0:T(8,128)(2,1)}, u32[]{:S(2)}, u32[]{:S(2)}) collective-permute-start(bf16[4,256,512]{2,1,0:T(8,128)(2,1)} %param.7), channel_id=1, source_target_pairs={{0,1},{1,0},{2,3},{3,2},{4,5},{5,4},{6,7},{7,6},{8,9},{9,8},{10,11... | collective-permute-start | bytes 3145736 | tf_op jit(solution)/shard_map/ppermute | solution.py:33
  3.6 61.3 %all-to-all-start = ((f32[64,1,64]{2,1,0:T(1,128)}), f32[64,1,64]{2,1,0:T(1,128)S(1)}, u32[]{:S(2)}, u32[]{:S(2)}) async-start(f32[64,1,64]{2,1,0:T(1,128)} %broadcast_in_dim.27), calls=%async_computation | async-start | bytes 65536 | tf_op jit(solution)/shard_map/all_to_all | solution.py:43
  38.9 6.6 %collective-permute-start.1 = (bf16[1,256,512]{2,1,0:T(8,128)(2,1)S(1)}, bf16[1,256,512]{2,1,0:T(8,128)(2,1)S(1)}, u32[]{:S(2)}, u32[]{:S(2)}) collective-permute-start(bf16[1,256,512]{2,1,0:T(8,128)(2,1)S(1)} %get-tuple-element.80), channel_id=1, source_target_pairs={{1,0},{2,1},{3,2},{4,3},{5,4},{6,5},{7,6},{8,7},{9,8},{10,9},{11,1... | collective-permute-start | bytes 786440 | tf_op jit(solution)/shard_map/ppermute | solution.py:51
  40.2 5.3 %collective-permute-start = (bf16[1,256,512]{2,1,0:T(8,128)(2,1)S(1)}, bf16[1,256,512]{2,1,0:T(8,128)(2,1)S(1)}, u32[]{:S(2)}, u32[]{:S(2)}) collective-permute-start(bf16[1,256,512]{2,1,0:T(8,128)(2,1)S(1)} %get-tuple-element.81), channel_id=1, source_target_pairs={{0,1},{1,2},{2,3},{3,4},{4,5},{5,6},{6,7},{7,8},{8,9},{9,10},{10,1... | collective-permute-start | bytes 786440 | tf_op jit(solution)/shard_map/ppermute | solution.py:50
  45.8 2.8 %slice-start = ((s8[4718592]{0:T(1024)(128)(4,1)}), s8[4194304]{0:T(1024)(128)(4,1)S(1)}, s32[]{:S(2)}) async-start(s8[4718592]{0:T(1024)(128)(4,1)} %bitcast.258), calls=%async_computation.1 | async-start | bytes 8388608
  45.8 2.8 %slice-start.1 = ((s8[4718592]{0:T(1024)(128)(4,1)}), s8[524288]{0:T(1024)(128)(4,1)S(1)}, s32[]{:S(2)}) async-start(s8[4718592]{0:T(1024)(128)(4,1)} %bitcast.258), calls=%async_computation.2 | async-start | bytes 1048576
  53.6 4.4 %collective-permute-start.2 = (bf16[256,1536]{1,0:T(8,128)(2,1)S(1)}, bf16[256,1536]{1,0:T(8,128)(2,1)S(1)}, u32[]{:S(2)}, u32[]{:S(2)}) collective-permute-start(bf16[256,1536]{1,0:T(8,128)(2,1)S(1)} %slice.571), channel_id=1, source_target_pairs={{0,1},{1,0},{2,3},{3,2},{4,5},{5,4},{6,7},{7,6},{8,9},{9,8},{10,11... | collective-permute-start | bytes 2359304 | tf_op jit(solution)/shard_map/ppermute | solution.py:33
  62.8 2.5 %copy-start.7 = (f32[512]{0:T(512)S(1)}, f32[512]{0:T(512)}, u32[]{:S(2)}) copy-start(f32[512]{0:T(512)} %param.10) | copy-start | bytes 6148
  62.8 2.5 %copy-start.10 = (f32[512]{0:T(512)S(1)}, f32[512]{0:T(512)}, u32[]{:S(2)}) copy-start(f32[512]{0:T(512)} %param.11) | copy-start | bytes 6148
  71.9 7.8 %copy-start.6 = (f16[9,3,8,512]{3,2,1,0:T(8,128)(2,1)}, f16[9,3,8,512]{3,2,1,0:T(8,128)(2,1)S(1)}, u32[]{:S(2)}) copy-start(f16[9,3,8,512]{3,2,1,0:T(8,128)(2,1)S(1)} %pad_maximum_fusion.12) | copy-start | bytes 663556
  79.1 7.4 %collective-permute-start.4 = (f32[2,512]{1,0:T(2,128)S(1)}, f32[2,512]{1,0:T(2,128)S(1)}, u32[]{:S(2)}, u32[]{:S(2)}) collective-permute-start(f32[2,512]{1,0:T(2,128)S(1)} %pad_maximum_fusion.20), channel_id=1, source_target_pairs={{0,1},{1,0},{2,3},{3,2},{4,5},{5,4},{6,7},{7,6},{8,9},{9,8},{10,11... | collective-permute-start | bytes 12296 | tf_op jit(solution)/shard_map/ppermute | solution.py:33
  80.1 6.7 %slice-start.2 = ((f16[9,3,8,512]{3,2,1,0:T(8,128)(2,1)}), f16[9,2,8,512]{3,2,1,0:T(8,128)(2,1)S(1)}, s32[]{:S(2)}) async-start(f16[9,3,8,512]{3,2,1,0:T(8,128)(2,1)} %copy-done.6), calls=%async_computation.3 | async-start | bytes 294912 | tf_op jit(solution)/shard_map/slice | solution.py:186
  80.3 38.0 %collective-permute-start.10 = (f16[9,9,8,512]{3,2,0,1:T(8,128)(2,1)S(1)}, f16[9,9,8,512]{3,2,0,1:T(8,128)(2,1)S(1)}, u32[]{:S(2)}, u32[]{:S(2)}) collective-permute-start(f16[9,9,8,512]{3,2,0,1:T(8,128)(2,1)S(1)} %copy.36), channel_id=1, source_target_pairs={{0,2},{2,4},{4,6},{6,8},{8,10},{10,12},{12,14},{14,16},{16,18},{18... | collective-permute-start | bytes 1990664 | tf_op jit(solution)/shard_map/ppermute | solution.py:38
  83.5 34.8 %collective-permute-start.9 = (f16[9,9,8,512]{3,2,0,1:T(8,128)(2,1)S(1)}, f16[9,9,8,512]{3,2,0,1:T(8,128)(2,1)S(1)}, u32[]{:S(2)}, u32[]{:S(2)}) collective-permute-start(f16[9,9,8,512]{3,2,0,1:T(8,128)(2,1)S(1)} %copy.35), channel_id=1, source_target_pairs={{0,62},{2,0},{4,2},{6,4},{8,6},{10,8},{12,10},{14,12},{16,14},{18,... | collective-permute-start | bytes 1990664 | tf_op jit(solution)/shard_map/ppermute | solution.py:38
  86.6 16.6 %collective-permute-start.6 = (f16[10,8,512]{2,1,0:T(8,128)(2,1)S(1)}, f16[10,8,512]{2,1,0:T(8,128)(2,1)S(1)}, u32[]{:S(2)}, u32[]{:S(2)}) collective-permute-start(f16[10,8,512]{2,1,0:T(8,128)(2,1)S(1)} %pad_maximum_fusion.16), channel_id=1, source_target_pairs={{0,2},{2,4},{4,6},{6,8},{8,10},{10,12},{12,14},{14,16},{16,18},{18... | collective-permute-start | bytes 245768 | tf_op jit(solution)/shard_map/ppermute | solution.py:38
  86.8 17.7 %collective-permute-start.5 = (f16[19,8,512]{2,1,0:T(8,128)(2,1)S(1)}, f16[19,8,512]{2,1,0:T(8,128)(2,1)S(1)}, u32[]{:S(2)}, u32[]{:S(2)}) collective-permute-start(f16[19,8,512]{2,1,0:T(8,128)(2,1)S(1)} %pad_maximum_fusion.15), channel_id=1, source_target_pairs={{0,62},{2,0},{4,2},{6,4},{8,6},{10,8},{12,10},{14,12},{16,14},{18,... | collective-permute-start | bytes 466952 | tf_op jit(solution)/shard_map/ppermute | solution.py:38
  104.8 9.9 %collective-permute-start.7 = (f16[10,8,512]{2,1,0:T(8,128)(2,1)S(1)}, f16[10,8,512]{2,1,0:T(8,128)(2,1)S(1)}, u32[]{:S(2)}, u32[]{:S(2)}) collective-permute-start(f16[10,8,512]{2,1,0:T(8,128)(2,1)S(1)} %pad_maximum_fusion.17), channel_id=1, source_target_pairs={{0,58},{2,60},{4,62},{6,0},{8,2},{10,4},{12,6},{14,8},{16,10},{18,... | collective-permute-start | bytes 245768 | tf_op jit(solution)/shard_map/ppermute | solution.py:38
  110.5 7.7 %collective-permute-start.8 = (f16[10,8,512]{2,1,0:T(8,128)(2,1)S(1)}, f16[10,8,512]{2,1,0:T(8,128)(2,1)S(1)}, u32[]{:S(2)}, u32[]{:S(2)}) collective-permute-start(f16[10,8,512]{2,1,0:T(8,128)(2,1)S(1)} %maximum_maximum_fusion), channel_id=1, source_target_pairs={{0,6},{2,8},{4,10},{6,12},{8,14},{10,16},{12,18},{14,20},{16,22},{... | collective-permute-start | bytes 245768 | tf_op jit(solution)/shard_map/ppermute | solution.py:38
  118.7 19.8 %collective-permute-start.11 = (f16[28,8,512]{2,1,0:T(8,128)(2,1)S(1)}, f16[28,8,512]{2,1,0:T(8,128)(2,1)S(1)}, u32[]{:S(2)}, u32[]{:S(2)}) collective-permute-start(f16[28,8,512]{2,1,0:T(8,128)(2,1)S(1)} %pad_maximum_fusion.10), channel_id=1, source_target_pairs={{0,58},{2,60},{4,62},{6,0},{8,2},{10,4},{12,6},{14,8},{16,10},{18,... | collective-permute-start | bytes 688136 | tf_op jit(solution)/shard_map/ppermute | solution.py:38
  126.8 17.7 %collective-permute-start.12 = (f16[28,8,512]{2,1,0:T(8,128)(2,1)S(1)}, f16[28,8,512]{2,1,0:T(8,128)(2,1)S(1)}, u32[]{:S(2)}, u32[]{:S(2)}) collective-permute-start(f16[28,8,512]{2,1,0:T(8,128)(2,1)S(1)} %pad_maximum_fusion.11), channel_id=1, source_target_pairs={{0,6},{2,8},{4,10},{6,12},{8,14},{10,16},{12,18},{14,20},{16,22},{... | collective-permute-start | bytes 688136 | tf_op jit(solution)/shard_map/ppermute | solution.py:38
  144.9 20.4 %collective-permute-start.14 = (f16[10,8,512]{2,1,0:T(8,128)(2,1)S(1)}, f16[10,8,512]{2,1,0:T(8,128)(2,1)S(1)}, u32[]{:S(2)}, u32[]{:S(2)}) collective-permute-start(f16[10,8,512]{2,1,0:T(8,128)(2,1)S(1)} %pad_maximum_fusion.19), channel_id=1, source_target_pairs={{0,18},{2,20},{4,22},{6,24},{8,26},{10,28},{12,30},{14,32},{16,34}... | collective-permute-start | bytes 245768 | tf_op jit(solution)/shard_map/ppermute | solution.py:38
  149.1 24.4 %collective-permute-start.13 = (f16[10,8,512]{2,1,0:T(8,128)(2,1)S(1)}, f16[10,8,512]{2,1,0:T(8,128)(2,1)S(1)}, u32[]{:S(2)}, u32[]{:S(2)}) collective-permute-start(f16[10,8,512]{2,1,0:T(8,128)(2,1)S(1)} %pad_maximum_fusion.18), channel_id=1, source_target_pairs={{0,46},{2,48},{4,50},{6,52},{8,54},{10,56},{12,58},{14,60},{16,62}... | collective-permute-start | bytes 245768 | tf_op jit(solution)/shard_map/ppermute | solution.py:38
  (7 other events, 11.8 us)
